TPU v7x, 512 devices: a whole 4x8x8 slice. The times are simulated.
512 devices in a mesh: grp: 8 (over z), dp: 64 (over y, x, core).
Axes of the slice: x: 4, y: 8, z: 8, core: 2. Of those that a mesh axis runs over, the one named last changes fastest.
Arguments:
- start_state: bfloat16 [65536, 512], P(('grp', 'dp')), may hold values from -24 to 24
- w_up: bfloat16 [512, 1024], replicated, may hold values from -0.25 to 0.25
- b_up: float32 [1024], replicated, may hold values from -3 to 3
- w_down: bfloat16 [1024, 512], replicated, may hold values from -0.1875 to 0.1875
- w_spread: bfloat16 [512, 1024], replicated, may hold values from -0.25 to 0.25
- w_scale: bfloat16 [1024, 512], replicated, may hold values from -0.1875 to 0.1875
- b_scale: float32 [512], replicated, may hold values from -4 to 4
- brownian_noise: bfloat16 [3, 65536, 512], P(None, ('grp', 'dp')), may hold values from -5 to 5
- step_mults: int32 [3, 65536], P(None, ('grp', 'dp')), may hold values from 1 to 4
- accept_flags: int32 [3, 65536], P(None, ('grp', 'dp')), may hold values 0 or 1
- cotangent: bfloat16 [65536, 512], P(('grp', 'dp')), may hold values from -6 to 6
Outputs:
- err_norms: float32 [3], replicated
- grad_up: float32 [512, 1024], P('dp')
- grad_down: float32 [512, 1024], P('dp')
All inputs are finite; a program needn't handle non-finite values. No bound on the sum of `accept_flags` on one device may be relied on, other than what follows from the above.
Results may differ from a plain program's by a relative error of at most 0.0033.
Values sent between devices are 32-bit elements; how exact they have to be, the bound alone decides.
No kernel may reach another device: no remote copies, remote signals or barrier semaphores. Data moves between devices by JAX's collectives and lax.ppermute only.
A program may use at most 64 MiB of HBM per device.

v0:
```python
import jax
import jax.numpy as jnp
from jax import lax
from jax.sharding import Mesh
from jax.sharding import PartitionSpec as P

DP = ("dp_0", "dp_1", "dp_2")
GRP_DP = ("grp", "dp_0", "dp_1", "dp_2")


base_step = 0.05
abs_tol = 0.01
rel_tol = 0.01


def copy_for_each(shard, axis):
    copies = jnp.broadcast_to(shard, (lax.axis_size(axis), *shard.shape))
    return lax.all_to_all(copies, axis, split_axis=0, concat_axis=0, tiled=True)


def taken_together(shard, axis):
    everything = copy_for_each(shard, axis)
    return jnp.sum(everything, axis=0)


def over_axes(shard, axes):
    far, near = axes
    return taken_together(taken_together(shard, near), far)


def in_blocks(shard, dim, size):
    before, after = (shard.shape[:dim], shard.shape[dim + 1 :])
    return jnp.moveaxis(shard.reshape(*before, size, -1, *after), dim, 0)


def summed_on_arrival(shard, axis, dim):
    size = lax.axis_size(axis)
    blocks = lax.all_to_all(in_blocks(shard, dim, size), axis, 0, 0, tiled=True)
    return jnp.sum(blocks, axis=0)


def sum_in_two_steps(shard, axes, dim):
    far, near = axes
    own = summed_on_arrival(in_blocks(shard, dim, lax.axis_size(far)), near, dim + 1)
    return jnp.sum(lax.all_to_all(own, far, 0, 0, tiled=True), axis=0)


def sent_together(arrays, axis, dim, along):
    widths = [a.shape[along] for a in arrays]
    both = jnp.concatenate(arrays, axis=along)
    filled = sum_in_two_steps(both, axis, dim)
    return tuple(jnp.split(filled, [sum(widths[:k]) for k in range(1, len(widths))], axis=along))


def together(arrays, axis):
    ravelled, at, finished = (jnp.concatenate([a.reshape(-1) for a in arrays]), 0, [])
    so_far = taken_together(ravelled, axis)
    for a in arrays:
        finished.append(so_far[at : at + a.size].reshape(a.shape))
        at += a.size
    return tuple(finished)


def diffuse(current, w_first, w_second, b_second):
    inner = jax.nn.silu(
        jnp.dot(current.astype(jnp.bfloat16), w_first, preferred_element_type=jnp.float32)
    )
    outer = jnp.dot(inner.astype(jnp.bfloat16), w_second, preferred_element_type=jnp.float32)
    return 0.6 * jax.nn.sigmoid(outer + b_second)


def forward_step(
    current, w_up, b_up, w_down, w_spread, w_scale, b_scale, noise_now, mult_now, flag_now
):
    low_state = current.astype(jnp.bfloat16)
    pre_act = jnp.dot(low_state, w_up, preferred_element_type=jnp.float32) + b_up
    hidden = jax.nn.silu(pre_act).astype(jnp.bfloat16)
    drift_out = jnp.dot(hidden, w_down, preferred_element_type=jnp.float32)
    step_size = mult_now.astype(jnp.float32)[:, None] * base_step
    sqrt_step = jnp.sqrt(step_size)
    brownian = sqrt_step * noise_now.astype(jnp.float32)
    keep_mask = flag_now.astype(jnp.float32)[:, None]

    def update(before):
        spread = diffuse(before, w_spread, w_scale, b_scale)
        shifted = diffuse(before + spread * sqrt_step, w_spread, w_scale, b_scale)
        milstein = (shifted - spread) * (brownian * brownian - step_size) / (2.0 * sqrt_step)
        proposal = before + drift_out * step_size + spread * brownian + milstein
        return (keep_mask * proposal + (1.0 - keep_mask) * before, milstein)

    (advanced, milstein), pull_back = jax.vjp(update, current)
    scaled = milstein / (abs_tol + rel_tol * jnp.abs(current))
    err_part = jnp.sum(scaled * scaled)
    return (advanced, err_part, (low_state, pre_act, hidden, pull_back, step_size, keep_mask))


def backward_step(cot_state, record, w_up, w_down, grad_up, grad_down):
    low_state, pre_act, hidden, pull_back, step_size, keep_mask = record
    cot_drift = (cot_state * keep_mask * step_size).astype(jnp.bfloat16)
    grad_down = grad_down + lax.dot_general(
        cot_drift, hidden, (((0,), (0,)), ((), ())), preferred_element_type=jnp.float32
    )
    sigma = jax.nn.sigmoid(pre_act)
    back_pre = lax.dot_general(
        cot_drift, w_down, (((1,), (1,)), ((), ())), preferred_element_type=jnp.float32
    )
    cot_pre = (back_pre * sigma * (1.0 + pre_act * (1.0 - sigma))).astype(jnp.bfloat16)
    grad_up = grad_up + lax.dot_general(
        low_state, cot_pre, (((0,), (0,)), ((), ())), preferred_element_type=jnp.float32
    )
    through = pull_back((cot_state, jnp.zeros_like(cot_state)))[0]
    cot_state = through + lax.dot_general(
        cot_pre, w_up, (((1,), (1,)), ((), ())), preferred_element_type=jnp.float32
    )
    return (cot_state, grad_up, grad_down)


def per_device(
    start_state,
    w_up,
    b_up,
    w_down,
    w_spread,
    w_scale,
    b_scale,
    brownian_noise,
    step_mults,
    accept_flags,
    cotangent,
):
    groups = lax.axis_size("grp")
    members = lax.axis_size(DP)
    row_count = start_state.shape[0] * start_state.shape[1] * groups * members
    step_count = brownian_noise.shape[0]
    current = start_state.astype(jnp.float32)
    records = []
    err_sums = []
    for step_index in range(step_count):
        current, err_part, record = forward_step(
            current,
            w_up,
            b_up,
            w_down,
            w_spread,
            w_scale,
            b_scale,
            brownian_noise[step_index],
            step_mults[step_index],
            accept_flags[step_index],
        )
        records.append(record)
        err_sums.append(err_part)
    totals = over_axes(jnp.stack(err_sums), (("grp", "dp_0"), ("dp_1", "dp_2")))
    err_norms = jnp.sqrt(totals / row_count)
    cot_state = cotangent.astype(jnp.float32)
    grad_up = jnp.zeros(w_up.shape, jnp.float32)
    grad_down = jnp.zeros((w_down.shape[1], w_down.shape[0]), jnp.float32)
    for step_index in reversed(range(step_count)):
        cot_state, grad_up, grad_down = backward_step(
            cot_state, records[step_index], w_up, w_down, grad_up, grad_down
        )
    inner_up, inner_down = sent_together((grad_up, grad_down), (("dp_0", "dp_1"), "dp_2"), 0, 1)
    grad_up, grad_down = together((inner_up, inner_down), "grp")
    return (err_norms, grad_up, grad_down)


def solution(mesh):
    split = Mesh(mesh.devices.reshape(mesh.shape["grp"], 8, 4, 2), ("grp", "dp_0", "dp_1", "dp_2"))
    return jax.shard_map(
        per_device,
        mesh=split,
        in_specs=(
            P(GRP_DP, None),
            P(),
            P(),
            P(),
            P(),
            P(),
            P(),
            P(None, GRP_DP, None),
            P(None, GRP_DP),
            P(None, GRP_DP),
            P(GRP_DP, None),
        ),
        out_specs=(P(), P(DP, None), P(DP, None)),
        check_vma=False,
    )
```

profile of v0, /device:TPU:2, one launch (start us, length us, event | category | flops | bytes accessed | tf_op | source)
XLA Modules:
  0.0 188.4 jit_solution(17318841570934697758)
XLA Ops:
  0.6 0.8 convert_bitcast_fusion
  1.5 1.3 broadcast_subtract_fusion
  2.8 1.3 multiply_bitcast_fusion
  4.1 0.8 broadcast_multiply_fusion.3
  4.9 1.5 convolution_add_fusion.2
  6.5 2.0 %fusion.48 = f32[128,512]{1,0:T(8,128)S(1)} fusion(bf16[1024,512]{1,0:T(8,128)(2,1)} %param.16, f32[512]{0:T(512)} %param.17, bf16[128,512]{1,0:T(8,128)(2,1)} %param.11, bf16[512,1024]{1,0:T(8,128)(2,1)S(1)} %copy-done), kind=kOutput, calls=%fused_computation.72 | convolution fusion | flops 269352960 | bytes 2492416 | tf_op jit(solution)/shard_map/jvp()/dot_general | solution.py:68
  8.6 2.0 %fusion.151 = (f32[]{:T(128)}, f32[128,512]{1,0:T(8,128)}) fusion(bf16[128,512]{1,0:T(8,128)(2,1)S(1)} %copy-done.12, f32[128]{0:T(128)S(1)} %get-tuple-element.26, f32[128]{0:T(128)S(1)} %get-tuple-element.22, bf16[3,128,512]{2,1,0:T(8,128)(2,1)S(1)} %copy-done.41, f32[128]{0:T(128)S(1)} %get-tuple-element.27, f32[128,512]{1,0:T(8,128)S(1)} %fusion.48, ...), kind=kOutput, calls=%fused_computation.195 | convolution fusion | flops 270663680 | bytes 3280900 | tf_op jit(solution)/shard_map/jvp()/dot_general | solution.py:68
  10.6 1.8 fusion.37
  12.5 0.3 convolution_add_fusion.1
  12.8 0.3 fusion.245
  13.1 0.6 copy-done.40
  13.7 0.4 fusion.32
  14.1 0.4 copy-done.13
  14.5 0.3 fusion.159
  14.9 0.4 fusion.28
  15.3 0.4 copy-done.14
  15.8 0.5 copy-done.11
  16.3 0.4 fusion.24
  16.7 0.3 convolution_add_fusion
  17.0 0.3 fusion.240
  17.4 0.4 fusion.19
  17.8 0.5 copy-done.15
  18.3 0.4 fusion.160
  18.7 0.2 copy-done.22
  18.9 0.1 copy-done.36
  19.0 2.9 %multiply_reduce_fusion = (f32[]{:T(128)}, f32[]{:T(128)}, f32[128,512]{1,0:T(8,128)}) fusion(f32[128,512]{1,0:T(8,128)S(1)} %fusion.37, f32[128,512]{1,0:T(8,128)S(1)} %fusion.32, f32[128,512]{1,0:T(8,128)S(1)} %fusion.28, f32[128]{0:T(128)S(1)} %copy-done.36, f32[128]{0:T(128)S(1)} %copy-done.33, f32[128]{0:T(128)S(1)} %copy-done.25, ...), kind=kOutput, calls=%fused_computation.181 | convolution fusion | flops 137101312 | bytes 3413000 | tf_op jit(solution)/shard_map/jvp()/dot_general | solution.py:68
  21.9 0.5 fusion.5
  22.4 0.1 copy-done.23
  22.5 3.1 %fusion.55 = f32[128,512]{1,0:T(8,128)} fusion(bf16[512,1024]{1,0:T(8,128)(2,1)S(1)} %copy-done, f32[128,1024]{1,0:T(8,128)} %copy-done.16, bf16[1024,512]{1,0:T(8,128)(2,1)} %param.16, f32[128,512]{1,0:T(8,128)} %get-tuple-element.28, bf16[128,512]{1,0:T(8,128)(2,1)} %param.21, f32[128]{0:T(128)S(1)} %get-tuple-element.18, f32[128]{0:T(128)} %copy-done.38, ...), kind=kOutput, calls=%fused_computation.83 | convolution fusion | flops 270794752 | bytes 3409920 | tf_op jit(solution)/shard_map/transpose(jvp())/dot_general | solution.py:66
  25.7 3.4 %fusion.54 = f32[128,512]{1,0:T(8,128)} fusion(bf16[512,1024]{1,0:T(8,128)(2,1)S(1)} %copy-done, f32[128,1024]{1,0:T(8,128)} %copy-done.15, bf16[1024,512]{1,0:T(8,128)(2,1)} %param.16, f32[128,512]{1,0:T(8,128)} %fusion.55, bf16[128,512]{1,0:T(8,128)(2,1)} %param.21, f32[128,512]{1,0:T(8,128)} %copy-done.18, f32[128]{0:T(128)} %get-tuple-element.15, ...), kind=kOutput, calls=%fused_computation.81 | convolution fusion | flops 271515648 | bytes 4066304 | tf_op jit(solution)/shard_map/transpose(jvp())/dot_general | solution.py:66
  29.0 2.1 %convolution_add_fusion.4 = f32[128,512]{1,0:T(8,128)} fusion(f32[128,512]{1,0:T(8,128)} %fusion.54, bf16[128,1024]{1,0:T(8,128)(2,1)S(1)} %fusion.5, bf16[512,1024]{1,0:T(8,128)(2,1)S(1)} %copy-done.1), kind=kOutput, calls=%fused_computation.27 | convolution fusion | flops 134283264 | bytes 1835008 | tf_op jit(solution)/shard_map/dot_general | solution.py:112
  31.2 3.2 %fusion.52 = f32[128,512]{1,0:T(8,128)} fusion(bf16[512,1024]{1,0:T(8,128)(2,1)S(1)} %copy-done, f32[128,1024]{1,0:T(8,128)} %copy-done.14, bf16[1024,512]{1,0:T(8,128)(2,1)} %param.16, f32[128,512]{1,0:T(8,128)} %copy-done.45, f32[128,512]{1,0:T(8,128)} %convolution_add_fusion.4, f32[128]{0:T(128)} %copy-done.29, f32[128]{0:T(128)} %copy-done.35, ...), kind=kOutput, calls=%fused_computation.78 | convolution fusion | flops 270729216 | bytes 3540992 | tf_op jit(solution)/shard_map/transpose(jvp())/dot_general | solution.py:66
  34.4 2.7 %fusion.4 = bf16[128,1024]{1,0:T(8,128)(2,1)} fusion(bf16[1024,512]{1,0:T(8,128)(2,1)} %param.14, f32[128,1024]{1,0:T(8,128)} %copy-done.6, f32[128,512]{1,0:T(8,128)} %convolution_add_fusion.4, f32[128]{0:T(128)} %copy-done.29, f32[128]{0:T(128)} %copy-done.32), kind=kOutput, calls=%fused_computation.14 | convolution fusion | flops 135593984 | bytes 2098176 | tf_op jit(solution)/shard_map/dot_general | solution.py:104
  37.2 1.9 %fusion.276 = f32[512,1024]{1,0:T(8,128)} fusion(f32[128,512]{1,0:T(8,128)S(1)} %copy-done.9, f32[128]{0:T(128)S(1)} %copy-done.30, f32[128]{0:T(128)S(1)} %copy-done.34, f32[128,1024]{1,0:T(8,128)S(1)} %copy-done.7), kind=kOutput, calls=%fused_computation.286 | convolution fusion | flops 135069696 | bytes 2884608 | tf_op jit(solution)/shard_map/dot_general | solution.py:100
  39.1 1.9 %fusion.83 = f32[512,1024]{1,0:T(8,128)} fusion(f32[128,1024]{1,0:T(8,128)S(1)} %convolution_add_fusion, bf16[128,512]{1,0:T(8,128)(2,1)S(1)} %copy-done.20, f32[128]{0:T(128)S(1)} %get-tuple-element.18, f32[128]{0:T(128)S(1)} %copy-done.23), kind=kOutput, calls=%fused_computation.136 | convolution fusion | flops 135135232 | bytes 2753536 | tf_op jit(solution)/shard_map/dot_general | solution.py:100
  41.0 1.8 fusion.237
  42.8 2.6 %fusion.51 = f32[128,512]{1,0:T(8,128)S(1)} fusion(bf16[512,1024]{1,0:T(8,128)(2,1)S(1)} %copy-done, f32[128,1024]{1,0:T(8,128)} %copy-done.13, bf16[1024,512]{1,0:T(8,128)(2,1)} %param.16, f32[128,512]{1,0:T(8,128)} %copy-done.17, f32[128,512]{1,0:T(8,128)} %fusion.52, f32[128,512]{1,0:T(8,128)S(1)} %copy-done.10, f32[128]{0:T(128)} %copy-done.37, ...), kind=kOutput, calls=%fused_computation.76 | convolution fusion | flops 271384576 | bytes 4328448 | tf_op jit(solution)/shard_map/transpose(jvp())/dot_general | solution.py:66
  45.5 1.9 fusion.242
  47.3 0.5 fusion.49
  47.9 0.6 copy-done.3
  48.4 3.0 %add_add_fusion = f32[512,1024]{1,0:T(8,128)} fusion(f32[512,1024]{1,0:T(8,128)S(1)} %copy-done.3, f32[512,1024]{1,0:T(8,128)S(1)} %copy-done.2, bf16[128,512]{1,0:T(8,128)(2,1)S(1)} %fusion.49, f32[128,1024]{1,0:T(8,128)} %copy-done.5), kind=kOutput, calls=%fused_computation.3 | convolution fusion | flops 135921664 | bytes 6946816 | tf_op jit(solution)/shard_map/dot_general | solution.py:100
  51.4 4.5 %bitcast_add_fusion = f32[512,1024]{1,0:T(8,128)} fusion(f32[512,1024]{1,0:T(8,128)S(1)} %copy-done.4, f32[512,1024]{1,0:T(8,128)} %fusion.242, bf16[128,512]{1,0:T(8,128)(2,1)S(1)} %copy-done.12, bf16[128,512]{1,0:T(8,128)(2,1)S(1)} %fusion.49, bf16[1024,512]{1,0:T(8,128)(2,1)} %param.14, f32[128,1024]{1,0:T(8,128)} %copy-done.5), kind=kOutput, calls=%fused_computation.2 | convolution fusion | flops 270663680 | bytes 8126464 | tf_op jit(solution)/shard_map/dot_general | solution.py:108
  55.9 2.7 %pad_maximum_fusion = f32[512,2048]{1,0:T(8,128)S(1)} fusion(f32[512,1024]{1,0:T(8,128)} %add_add_fusion, f32[512,1024]{1,0:T(8,128)} %bitcast_add_fusion), kind=kLoop, calls=%fused_computation | loop fusion | flops 1048576 | bytes 8388608 | tf_op jit(solution)/shard_map/concatenate | solution.py:50
  58.6 2.5 %copy.40 = f32[32,2,8,2048]{3,2,0,1:T(8,128)} copy(f32[32,2,8,2048]{3,2,1,0:T(8,128)S(1)} %bitcast.121) | data formatting | bytes 8388608 | tf_op jit(solution)/shard_map/reshape;reshape | solution.py:33
  61.2 5.6 %all-to-all-start.2 = ((f32[2,32,8,2048]{3,2,1,0:T(8,128)}), f32[2,32,8,2048]{3,2,1,0:T(8,128)}, u32[]{:S(2)}, u32[]{:S(2)}) async-start(f32[2,32,8,2048]{3,2,1,0:T(8,128)} %bitcast.120), calls=%async_computation.2 | async-start | bytes 8388608 | tf_op jit(solution)/shard_map/all_to_all | solution.py:38
  66.8 2.0 %pad_maximum_fusion.2 = f32[3]{0:T(128)S(1)} fusion(f32[1]{0:T(128)} %bitcast.10, f32[1]{0:T(128)} %bitcast.6, f32[1]{0:T(128)} %bitcast.2), kind=kLoop, calls=%fused_computation.240 | loop fusion | flops 6 | bytes 24 | tf_op jit(solution)/shard_map/stack | solution.py:153
  68.8 2.5 %all-to-all-done.2 = f32[2,32,8,2048]{3,2,1,0:T(8,128)} async-done(((f32[2,32,8,2048]{3,2,1,0:T(8,128)}), f32[2,32,8,2048]{3,2,1,0:T(8,128)}, u32[]{:S(2)}, u32[]{:S(2)}) %all-to-all-start.2) | async-done | bytes 4194336 | tf_op jit(solution)/shard_map/all_to_all | solution.py:38
  71.3 0.6 broadcast_in_dim.6
  71.9 9.1 %all-to-all-start = ((f32[8,1,3]{2,1,0:T(1,128)}), f32[8,1,3]{2,1,0:T(1,128)S(1)}, u32[]{:S(2)}, u32[]{:S(2)}) async-start(f32[8,1,3]{2,1,0:T(1,128)} %broadcast_in_dim.6), calls=%async_computation | async-start | bytes 8192 | tf_op jit(solution)/shard_map/all_to_all | solution.py:18
  81.0 4.1 %reduce_sum.77 = f32[32,8,2048]{2,1,0:T(8,128)} reduce(f32[2,32,8,2048]{3,2,1,0:T(8,128)} %all-to-all-done.2, f32[]{:T(128)} %constant.27.clone.1), dimensions={0}, to_apply=%region_5.6 | reduce | flops 524288 | bytes 6291460 | tf_op jit(solution)/shard_map/reduce_sum | solution.py:39
  85.1 6.0 %all-to-all-start.3 = ((f32[32,8,2048]{2,1,0:T(8,128)}), f32[32,8,2048]{2,1,0:T(8,128)S(1)}, u32[]{:S(2)}, u32[]{:S(2)}) async-start(f32[32,8,2048]{2,1,0:T(8,128)} %reduce_sum.77), calls=%async_computation.3 | async-start | bytes 4194304 | tf_op jit(solution)/shard_map/all_to_all | solution.py:45
  91.1 49.5 %all-to-all-done.3 = f32[32,8,2048]{2,1,0:T(8,128)S(1)} async-done(((f32[32,8,2048]{2,1,0:T(8,128)}), f32[32,8,2048]{2,1,0:T(8,128)S(1)}, u32[]{:S(2)}, u32[]{:S(2)}) %all-to-all-start.3) | async-done | bytes 2097184 | tf_op jit(solution)/shard_map/all_to_all | solution.py:45
  140.6 0.6 broadcast_in_dim.7
  141.2 13.5 %all-to-all-start.1 = ((f32[64,1,3]{2,1,0:T(1,128)}), f32[64,1,3]{2,1,0:T(1,128)S(1)}, u32[]{:S(2)}, u32[]{:S(2)}) async-start(f32[64,1,3]{2,1,0:T(1,128)} %broadcast_in_dim.7), calls=%async_computation.1 | async-start | bytes 65536 | tf_op jit(solution)/shard_map/all_to_all | solution.py:18
  154.7 0.1 reduce_sum.78
  154.9 11.8 %all-to-all-done.1 = f32[64,1,3]{2,1,0:T(1,128)S(1)} async-done(((f32[64,1,3]{2,1,0:T(1,128)}), f32[64,1,3]{2,1,0:T(1,128)S(1)}, u32[]{:S(2)}, u32[]{:S(2)}) %all-to-all-start.1) | async-done | bytes 800 | tf_op jit(solution)/shard_map/all_to_all | solution.py:18
  166.7 1.1 broadcast_in_dim.8
  167.7 3.5 %all-to-all-start.4 = ((f32[8,1,16384]{2,1,0:T(1,128)}), f32[8,1,16384]{2,1,0:T(1,128)S(1)}, u32[]{:S(2)}, u32[]{:S(2)}) async-start(f32[8,1,16384]{2,1,0:T(1,128)} %broadcast_in_dim.8), calls=%async_computation.4 | async-start | bytes 1048576 | tf_op jit(solution)/shard_map/all_to_all | solution.py:18
  171.2 0.1 reduce_sum.76
  171.3 0.5 multiply_sqrt_fusion
  171.8 14.9 %all-to-all-done.4 = f32[8,1,16384]{2,1,0:T(1,128)S(1)} async-done(((f32[8,1,16384]{2,1,0:T(1,128)}), f32[8,1,16384]{2,1,0:T(1,128)S(1)}, u32[]{:S(2)}, u32[]{:S(2)}) %all-to-all-start.4) | async-done | bytes 524320 | tf_op jit(solution)/shard_map/all_to_all | solution.py:18
  186.7 0.4 reduce_sum.79
  187.2 0.6 slice.65
  187.8 0.6 slice.63
  (92 shorter events, 0.3 us)
Async XLA Ops:
  0.6 5.8 %copy-start = (bf16[512,1024]{1,0:T(8,128)(2,1)S(1)}, bf16[512,1024]{1,0:T(8,128)(2,1)}, u32[]{:S(2)}) copy-start(bf16[512,1024]{1,0:T(8,128)(2,1)} %param.15) | copy-start | bytes 3145732
  1.5 14.3 %copy-start.29 = (f32[128]{0:T(128)}, f32[128]{0:T(128)S(1)}, u32[]{:S(2)}) copy-start(f32[128]{0:T(128)S(1)} %get-tuple-element.20) | copy-start | bytes 1540
  2.8 13.0 %copy-start.37 = (f32[128]{0:T(128)}, f32[128]{0:T(128)S(1)}, u32[]{:S(2)}) copy-start(f32[128]{0:T(128)S(1)} %get-tuple-element.16) | copy-start | bytes 1540
  4.1 11.6 %copy-start.32 = (f32[128]{0:T(128)}, f32[128]{0:T(128)S(1)}, u32[]{:S(2)}) copy-start(f32[128]{0:T(128)S(1)} %get-tuple-element.23) | copy-start | bytes 1540
  4.9 9.6 %copy-start.27 = (f32[128]{0:T(128)}, f32[128]{0:T(128)S(1)}, u32[]{:S(2)}) copy-start(f32[128]{0:T(128)S(1)} %get-tuple-element.6) | copy-start | bytes 1540
  4.9 10.8 %copy-start.24 = (f32[128]{0:T(128)}, f32[128]{0:T(128)S(1)}, u32[]{:S(2)}) copy-start(f32[128]{0:T(128)S(1)} %get-tuple-element.25) | copy-start | bytes 1540
  4.9 10.8 %copy-start.35 = (f32[128]{0:T(128)}, f32[128]{0:T(128)S(1)}, u32[]{:S(2)}) copy-start(f32[128]{0:T(128)S(1)} %get-tuple-element.24) | copy-start | bytes 1540
  6.5 4.1 %copy-start.5 = (f32[128,1024]{1,0:T(8,128)}, f32[128,1024]{1,0:T(8,128)S(1)}, u32[]{:S(2)}) copy-start(f32[128,1024]{1,0:T(8,128)S(1)} %convolution_add_fusion.2) | copy-start | bytes 1572868
  6.5 2.1 %copy-start.12 = (bf16[128,512]{1,0:T(8,128)(2,1)S(1)}, bf16[128,512]{1,0:T(8,128)(2,1)}, u32[]{:S(2)}) copy-start(bf16[128,512]{1,0:T(8,128)(2,1)} %param.11) | copy-start | bytes 393220
  6.5 2.1 %copy-start.39 = (bf16[1024,512]{1,0:T(8,128)(2,1)S(1)}, bf16[1024,512]{1,0:T(8,128)(2,1)}, u32[]{:S(2)}) copy-start(bf16[1024,512]{1,0:T(8,128)(2,1)} %param.16) | copy-start | bytes 3145732
  6.5 2.1 %copy-start.41 = (bf16[3,128,512]{2,1,0:T(8,128)(2,1)S(1)}, bf16[3,128,512]{2,1,0:T(8,128)(2,1)}, u32[]{:S(2)}) copy-start(bf16[3,128,512]{2,1,0:T(8,128)(2,1)} %param.18) | copy-start | bytes 1179652
  6.5 2.1 %copy-start.42 = (f32[512]{0:T(512)S(1)}, f32[512]{0:T(512)}, u32[]{:S(2)}) copy-start(f32[512]{0:T(512)} %param.17) | copy-start | bytes 6148
  8.6 2.0 %copy-start.44 = (f32[128,512]{1,0:T(8,128)}, f32[128,512]{1,0:T(8,128)S(1)}, u32[]{:S(2)}) copy-start(f32[128,512]{1,0:T(8,128)S(1)} %fusion.48) | copy-start | bytes 786436
  10.6 1.8 copy-start.1
  10.6 1.8 copy-start.21
  12.5 1.2 copy-start.40
  12.8 3.0 %copy-start.6 = (f32[128,1024]{1,0:T(8,128)}, f32[128,1024]{1,0:T(8,128)S(1)}, u32[]{:S(2)}) copy-start(f32[128,1024]{1,0:T(8,128)S(1)} %convolution_add_fusion.1) | copy-start | bytes 1572868
  13.7 0.8 copy-start.13
  14.5 4.1 %copy-start.17 = (f32[128,512]{1,0:T(8,128)}, f32[128,512]{1,0:T(8,128)S(1)}, u32[]{:S(2)}) copy-start(f32[128,512]{1,0:T(8,128)S(1)} %fusion.32) | copy-start | bytes 786436
  14.5 4.1 %copy-start.38 = (f32[128]{0:T(128)}, f32[128]{0:T(128)S(1)}, u32[]{:S(2)}) copy-start(f32[128]{0:T(128)S(1)} %get-tuple-element.31) | copy-start | bytes 1540
  14.9 0.8 copy-start.14
  14.9 1.4 copy-start.11
  15.7 2.9 %copy-start.45 = (f32[128,512]{1,0:T(8,128)}, f32[128,512]{1,0:T(8,128)S(1)}, u32[]{:S(2)}) copy-start(f32[128,512]{1,0:T(8,128)S(1)} %fusion.28) | copy-start | bytes 786436
  16.7 0.7 copy-start.43
  17.4 0.8 copy-start.15
  18.2 3.6 %copy-start.18 = (f32[128,512]{1,0:T(8,128)}, f32[128,512]{1,0:T(8,128)S(1)}, u32[]{:S(2)}) copy-start(f32[128,512]{1,0:T(8,128)S(1)} %fusion.19) | copy-start | bytes 786436
  18.2 0.7 copy-start.22
  18.2 0.7 copy-start.25
  18.2 0.7 copy-start.28
  18.2 0.7 copy-start.33
  18.3 0.7 copy-start.36
  18.6 3.3 %copy-start.16 = (f32[128,1024]{1,0:T(8,128)}, f32[128,1024]{1,0:T(8,128)S(1)}, u32[]{:S(2)}) copy-start(f32[128,1024]{1,0:T(8,128)S(1)} %fusion.160) | copy-start | bytes 1572868
  19.0 2.9 %copy-start.19 = (bf16[128,512]{1,0:T(8,128)(2,1)S(1)}, bf16[128,512]{1,0:T(8,128)(2,1)}, u32[]{:S(2)}) copy-start(bf16[128,512]{1,0:T(8,128)(2,1)} %param.21) | copy-start | bytes 393220
  21.9 0.7 copy-start.23
  34.4 2.8 %copy-start.7 = (f32[128,1024]{1,0:T(8,128)S(1)}, f32[128,1024]{1,0:T(8,128)}, u32[]{:S(2)}) copy-start(f32[128,1024]{1,0:T(8,128)} %copy-done.6) | copy-start | bytes 1572868
  34.4 2.8 %copy-start.9 = (f32[128,512]{1,0:T(8,128)S(1)}, f32[128,512]{1,0:T(8,128)}, u32[]{:S(2)}) copy-start(f32[128,512]{1,0:T(8,128)} %convolution_add_fusion.4) | copy-start | bytes 786436
  34.4 2.8 %copy-start.30 = (f32[128]{0:T(128)S(1)}, f32[128]{0:T(128)}, u32[]{:S(2)}) copy-start(f32[128]{0:T(128)} %copy-done.29) | copy-start | bytes 1540
  34.4 2.8 %copy-start.34 = (f32[128]{0:T(128)S(1)}, f32[128]{0:T(128)}, u32[]{:S(2)}) copy-start(f32[128]{0:T(128)} %copy-done.32) | copy-start | bytes 1540
  37.1 1.9 %copy-start.20 = (bf16[128,512]{1,0:T(8,128)(2,1)S(1)}, bf16[128,512]{1,0:T(8,128)(2,1)}, u32[]{:S(2)}) copy-start(bf16[128,512]{1,0:T(8,128)(2,1)} %param.21) | copy-start | bytes 393220
  41.0 1.8 copy-start.10
  41.0 1.8 copy-start.26
  41.0 1.8 copy-start.31
  42.8 2.6 %copy-start.8 = (bf16[128,1024]{1,0:T(8,128)(2,1)S(1)}, bf16[128,1024]{1,0:T(8,128)(2,1)}, u32[]{:S(2)}) copy-start(bf16[128,1024]{1,0:T(8,128)(2,1)} %fusion.4) | copy-start | bytes 786436
  45.4 2.4 %copy-start.2 = (f32[512,1024]{1,0:T(8,128)S(1)}, f32[512,1024]{1,0:T(8,128)}, u32[]{:S(2)}) copy-start(f32[512,1024]{1,0:T(8,128)} %fusion.276) | copy-start | bytes 6291460
  45.5 3.0 %copy-start.3 = (f32[512,1024]{1,0:T(8,128)S(1)}, f32[512,1024]{1,0:T(8,128)}, u32[]{:S(2)}) copy-start(f32[512,1024]{1,0:T(8,128)} %fusion.83) | copy-start | bytes 6291460
  48.4 3.0 %copy-start.4 = (f32[512,1024]{1,0:T(8,128)S(1)}, f32[512,1024]{1,0:T(8,128)}, u32[]{:S(2)}) copy-start(f32[512,1024]{1,0:T(8,128)} %fusion.237) | copy-start | bytes 6291460
  61.2 10.1 %all-to-all-start.2 = ((f32[2,32,8,2048]{3,2,1,0:T(8,128)}), f32[2,32,8,2048]{3,2,1,0:T(8,128)}, u32[]{:S(2)}, u32[]{:S(2)}) async-start(f32[2,32,8,2048]{3,2,1,0:T(8,128)} %bitcast.120), calls=%async_computation.2 | async-start | bytes 8388608 | tf_op jit(solution)/shard_map/all_to_all | solution.py:38
  71.9 13.2 %all-to-all-start = ((f32[8,1,3]{2,1,0:T(1,128)}), f32[8,1,3]{2,1,0:T(1,128)S(1)}, u32[]{:S(2)}, u32[]{:S(2)}) async-start(f32[8,1,3]{2,1,0:T(1,128)} %broadcast_in_dim.6), calls=%async_computation | async-start | bytes 8192 | tf_op jit(solution)/shard_map/all_to_all | solution.py:18
  85.1 55.5 %all-to-all-start.3 = ((f32[32,8,2048]{2,1,0:T(8,128)}), f32[32,8,2048]{2,1,0:T(8,128)S(1)}, u32[]{:S(2)}, u32[]{:S(2)}) async-start(f32[32,8,2048]{2,1,0:T(8,128)} %reduce_sum.77), calls=%async_computation.3 | async-start | bytes 4194304 | tf_op jit(solution)/shard_map/all_to_all | solution.py:45
  141.2 25.5 %all-to-all-start.1 = ((f32[64,1,3]{2,1,0:T(1,128)}), f32[64,1,3]{2,1,0:T(1,128)S(1)}, u32[]{:S(2)}, u32[]{:S(2)}) async-start(f32[64,1,3]{2,1,0:T(1,128)} %broadcast_in_dim.7), calls=%async_computation.1 | async-start | bytes 65536 | tf_op jit(solution)/shard_map/all_to_all | solution.py:18
  167.7 19.0 %all-to-all-start.4 = ((f32[8,1,16384]{2,1,0:T(1,128)}), f32[8,1,16384]{2,1,0:T(1,128)S(1)}, u32[]{:S(2)}, u32[]{:S(2)}) async-start(f32[8,1,16384]{2,1,0:T(1,128)} %broadcast_in_dim.8), calls=%async_computation.4 | async-start | bytes 1048576 | tf_op jit(solution)/shard_map/all_to_all | solution.py:18
where the time goes:
time: 189 us; the launch traced here: 188 us
  waiting for transfers between devices  78.6 us (42%)
  matrix products  46.9 us (25%)
  starting transfers between devices  37.7 us (20%)
  other arithmetic  14.2 us (8%)
  local copies, waits for them, and re-layouts  9.76 us (5%)
    all_to_all x1, waiting for transfers between devices, sum_in_two_steps(): return jnp.sum(lax.all_to_all(own, far, 0, 0, tiled=True), axis=0)  49.5 us
    all_to_all x3, waiting for transfers between devices, copy_for_each(): return lax.all_to_all(copies, axis, split_axis=0, concat_axis=0, tiled=True)  26.7 us
    all_to_all x3, starting transfers between devices, copy_for_each(): return lax.all_to_all(copies, axis, split_axis=0, concat_axis=0, tiled=True)  26.1 us
    dot_general x8, matrix products, diffuse(): jnp.dot(current.astype(jnp.bfloat16), w_first, preferred_element_type=jnp...  13.6 us
    dot_general x3, matrix products, backward_step(): lax.dot_general(low_state, cot_pre, (((0,), (0,)), ((), ())), preferred_e...  8.15 us
    dot_general x6, matrix products, diffuse(): jnp.dot(inner.astype(jnp.bfloat16), w_second, preferred_element_type=jnp....  8.05 us
    dot_general x3, matrix products, backward_step(): lax.dot_general(cot_drift, hidden, (((0,), (0,)), ((), ())), preferred_el...  6.84 us
    all_to_all x1, starting transfers between devices, sum_in_two_steps(): return jnp.sum(lax.all_to_all(own, far, 0, 0, tiled=True), axis=0)  5.95 us
  transfers between devices with their start and end apart: 5, of which 4 were waited for; matrix products, arithmetic and copies ran while one was open for 4% of the time, Pallas kernels for 0%

commit v1 on v0

v1 whole, which is shorter than its diff:
```python
import jax
import jax.numpy as jnp
from jax import lax
from jax.experimental import pallas as pl
from jax.experimental.pallas import tpu as pltpu
from jax.sharding import Mesh
from jax.sharding import PartitionSpec as P

DP = ("dp_0", "dp_1", "dp_2")
GRP_DP = ("grp", "dp_0", "dp_1", "dp_2")

base_step = 0.05
abs_tol = 0.01
rel_tol = 0.01
F32 = jnp.float32
BF16 = jnp.bfloat16


def mm(a, b):
    return jnp.dot(a, b, preferred_element_type=F32)


def mm_t(a, b):
    return lax.dot_general(a, b, (((1,), (1,)), ((), ())), preferred_element_type=F32)


def t_mm(a, b):
    return lax.dot_general(a, b, (((0,), (0,)), ((), ())), preferred_element_type=F32)


def sigmoid(x):
    return 0.5 * jnp.tanh(0.5 * x) + 0.5


def steps_kernel(
    core_ref,
    start_hbm, w_up_hbm, b_up_ref, w_down_hbm, w_spread_hbm, w_scale_hbm, b_scale_ref,
    noise_hbm, mults_ref, flags_ref, cot_hbm,
    keep_hbm, send_hbm, err_ref,
    start_v, w_up, w_down, w_spread, w_scale, noise_v, cot_v,
    d_pre, d_one, d_two, hid_v, low_v, cpre_v, cdrift_v, d_g, d_gbar, fac_v, dw_v, out_v,
    in_sems, out_sems,
):
    steps, rows, latent = noise_v.shape
    far, near = out_v.shape[1], out_v.shape[2]
    loads = {}
    for slot, (name, src, dst) in enumerate((
        ("start", start_hbm, start_v),
        ("spread", w_spread_hbm, w_spread),
        ("scale", w_scale_hbm, w_scale),
        ("up", w_up_hbm, w_up),
        ("noise", noise_hbm, noise_v),
        ("down", w_down_hbm, w_down),
        ("cot", cot_hbm, cot_v),
    )):
        loads[name] = pltpu.make_async_copy(src, dst, in_sems.at[slot])
        loads[name].start()

    per_row = jnp.concatenate(
        [
            mults_ref[...].astype(F32) * base_step,
            flags_ref[...].astype(F32),
            jnp.zeros((8 - 2 * steps, rows), F32),
        ],
        axis=0,
    )
    columns = jnp.transpose(per_row)
    b_up = b_up_ref[...]
    b_scale = b_scale_ref[...]

    loads["start"].wait()
    state = start_v[...].astype(F32)
    waited = {"start"}

    def need(name):
        if name not in waited:
            waited.add(name)
            loads[name].wait()

    def gated(pre):
        sig = sigmoid(pre)
        return (pre * sig).astype(BF16), sig * (1.0 + pre * (1.0 - sig))

    err_parts = []
    for n in range(steps):
        h = columns[:, n : n + 1]
        keep = columns[:, steps + n : steps + n + 1]
        root = jnp.sqrt(h)
        low = state.astype(BF16)
        low_v[n * rows : (n + 1) * rows, :] = low
        need("spread")
        inner, slope = gated(mm(low, w_spread[...]))
        d_one[n] = slope
        need("scale")
        sig_g = sigmoid(mm(inner, w_scale[...]) + b_scale)
        spread = 0.6 * sig_g
        d_g[n] = spread * (1.0 - sig_g)
        shifted_low = (state + spread * root).astype(BF16)
        inner, slope = gated(mm(shifted_low, w_spread[...]))
        d_two[n] = slope
        sig_s = sigmoid(mm(inner, w_scale[...]) + b_scale)
        shifted = 0.6 * sig_s
        d_gbar[n] = shifted * (1.0 - sig_s)
        need("up")
        hidden, slope = gated(mm(low, w_up[...]) + b_up)
        hid_v[n * rows : (n + 1) * rows, :] = hidden
        d_pre[n] = slope
        need("noise")
        brownian = root * noise_v[n].astype(F32)
        factor = (brownian * brownian - h) / (2.0 * root)
        dw_v[n] = brownian
        fac_v[n] = factor
        milstein = (shifted - spread) * factor
        scaled = milstein / (abs_tol + rel_tol * jnp.abs(state))
        err_parts.append(jnp.sum((scaled * scaled).reshape(rows // 8, 8, latent), axis=0))
        if n + 1 < steps:
            need("down")
            drift = mm(hidden, w_down[...])
            proposal = state + drift * h + spread * brownian + milstein
            state = keep * proposal + (1.0 - keep) * state

    err_rows = [jnp.sum(jnp.sum(p, axis=0, keepdims=True), axis=1, keepdims=True) for p in err_parts]
    row = lax.broadcasted_iota(jnp.int32, err_ref.shape, 0)
    err = jnp.zeros(err_ref.shape, F32)
    for n in range(steps):
        err = jnp.where(row == n, err_rows[n], err)
    err_ref[...] = err

    need("down")
    need("cot")
    cot = cot_v[...].astype(F32)

    def through_net(d_out, slope):
        d_inner = mm_t(d_out.astype(BF16), w_scale[...]).astype(BF16).astype(F32)
        return mm_t((d_inner * slope).astype(BF16), w_spread[...]).astype(BF16).astype(F32)

    for n in reversed(range(steps)):
        h = columns[:, n : n + 1]
        keep = columns[:, steps + n : steps + n + 1]
        root = jnp.sqrt(h)
        kept = cot * keep
        cdrift = (kept * h).astype(BF16)
        cdrift_v[n * rows : (n + 1) * rows, :] = cdrift
        cpre = (mm_t(cdrift, w_down[...]) * d_pre[n]).astype(BF16)
        cpre_v[n * rows : (n + 1) * rows, :] = cpre
        if n > 0:
            d_shift = kept * fac_v[n]
            d_state = through_net(d_shift * d_gbar[n], d_two[n])
            d_spread = kept * dw_v[n] - d_shift + d_state * root
            d_first = through_net(d_spread * d_g[n], d_one[n])
            cot = (kept + (1.0 - keep) * cot) + d_state + d_first + mm_t(cpre, w_up[...])

    tiles = w_up.shape[1] // 128

    def place(grad, first):
        for block in range(latent // 8):
            core = block % 2
            at = (block // 2) % far
            up = block // (2 * far)
            for t in range(tiles):
                out_v[core, at, up, (first + t) * 8 : (first + t + 1) * 8, :] = grad[
                    block * 8 : (block + 1) * 8, t * 128 : (t + 1) * 128
                ]

    place(t_mm(cdrift_v[...], hid_v[...]), tiles)
    place(t_mm(low_v[...], cpre_v[...]), 0)
    own = core_ref[0]
    out = pltpu.make_async_copy(out_v.at[1 - own], send_hbm, out_sems.at[0])
    stay = pltpu.make_async_copy(out_v.at[own], keep_hbm, out_sems.at[1])
    out.start()
    stay.start()
    out.wait()
    stay.wait()


def run_steps(core, *args):
    start, w_up, _, _, _, _, _, noise, _, _, _ = args
    steps, rows, latent = noise.shape
    wide = w_up.shape[1]
    far = lax.axis_size("dp_1")
    near = lax.axis_size("dp_0")
    block = (far, near, 2 * wide // 16, 128)
    hbm = pl.BlockSpec(memory_space=pl.ANY)
    vmem = pl.BlockSpec(memory_space=pltpu.VMEM)
    smem = pl.BlockSpec(memory_space=pltpu.SMEM)
    half = jax.ShapeDtypeStruct((far, near, 2 * wide // 16, 128), F32)
    del block
    half = jax.ShapeDtypeStruct((far, near, wide // 8, 128), F32)
    return pl.pallas_call(
        steps_kernel,
        out_shape=(half, half, jax.ShapeDtypeStruct((8, 128), F32)),
        in_specs=[smem, hbm, hbm, vmem, hbm, hbm, hbm, vmem, hbm, vmem, vmem, hbm],
        out_specs=(hbm, hbm, vmem),
        scratch_shapes=[
            pltpu.VMEM((rows, latent), BF16),
            pltpu.VMEM((latent, wide), BF16),
            pltpu.VMEM((wide, latent), BF16),
            pltpu.VMEM((latent, wide), BF16),
            pltpu.VMEM((wide, latent), BF16),
            pltpu.VMEM((steps, rows, latent), BF16),
            pltpu.VMEM((rows, latent), BF16),
            pltpu.VMEM((steps, rows, wide), F32),
            pltpu.VMEM((steps, rows, wide), F32),
            pltpu.VMEM((steps, rows, wide), F32),
            pltpu.VMEM((steps * rows, wide), BF16),
            pltpu.VMEM((steps * rows, latent), BF16),
            pltpu.VMEM((steps * rows, wide), BF16),
            pltpu.VMEM((steps * rows, latent), BF16),
            pltpu.VMEM((steps, rows, latent), F32),
            pltpu.VMEM((steps, rows, latent), F32),
            pltpu.VMEM((steps, rows, latent), F32),
            pltpu.VMEM((steps, rows, latent), F32),
            pltpu.VMEM((2, far, near, wide // 8, 128), F32),
            pltpu.SemaphoreType.DMA((7,)),
            pltpu.SemaphoreType.DMA((2,)),
        ],
        compiler_params=pltpu.CompilerParams(vmem_limit_bytes=60 * 1024 * 1024),
        name="milstein_steps",
    )(core, *args)


def swap_sum(value, axis, distance):
    size = lax.axis_size(axis)
    pairs = [(k, (k + distance) % size) for k in range(size)]
    return value + lax.ppermute(value, axis, pairs)


def per_device(
    start_state, w_up, b_up, w_down, w_spread, w_scale, b_scale,
    brownian_noise, step_mults, accept_flags, cotangent,
):
    groups = lax.axis_size("grp")
    members = lax.axis_size(DP)
    far = lax.axis_size("dp_1")
    near = lax.axis_size("dp_0")
    row_count = start_state.shape[0] * start_state.shape[1] * groups * members
    wide = w_up.shape[1]
    core = lax.axis_index("dp_2")[None]
    keep, send, err = run_steps(
        core, start_state, w_up, b_up[None], w_down, w_spread, w_scale, b_scale[None],
        brownian_noise, step_mults, accept_flags, cotangent,
    )
    mine = keep + lax.ppermute(send, "dp_2", [(0, 1), (1, 0)])
    parts = lax.all_to_all(mine, "dp_1", 0, 0, tiled=True)
    column = jnp.sum(parts, axis=0)
    pieces = column.reshape(near * groups, -1, 128)
    arrived = lax.all_to_all(pieces, ("dp_0", "grp"), 0, 0, tiled=True)
    piece = jnp.sum(arrived, axis=0)
    copies = jnp.broadcast_to(piece, (groups, *piece.shape))
    whole = lax.all_to_all(copies, "grp", 0, 0, tiled=True)
    grads = whole.reshape(2, wide // 128, 8, 128).transpose(0, 2, 1, 3).reshape(2, 8, wide)

    for axis in ("dp_2", "dp_1", "dp_0", "grp"):
        distance = 1
        while distance < lax.axis_size(axis):
            err = swap_sum(err, axis, distance)
            distance *= 2
    err_norms = jnp.sqrt(err[: brownian_noise.shape[0], 0] / row_count)
    return (err_norms, grads[0], grads[1])


def solution(mesh):
    split = Mesh(mesh.devices.reshape(mesh.shape["grp"], 8, 4, 2), ("grp", "dp_0", "dp_1", "dp_2"))
    return jax.shard_map(
        per_device,
        mesh=split,
        in_specs=(
            P(GRP_DP, None), P(), P(), P(), P(), P(), P(),
            P(None, GRP_DP, None), P(None, GRP_DP), P(None, GRP_DP), P(GRP_DP, None),
        ),
        out_specs=(P(), P(DP, None), P(DP, None)),
        check_vma=False,
    )
```

time: 189 us -> 148 us (0.78)
  the two profiles are of different devices: /device:TPU:2 before, /device:TPU:32 now
where the time goes in v1:
time: 148 us
  starting transfers between devices  48.3 us (33%)
  waiting for transfers between devices  47.3 us (32%)
  blocking collectives  30.7 us (21%)
  Pallas kernels  15.7 us (11%)
  other arithmetic  3.58 us (2%)
    ppermute x9, waiting for transfers between devices, swap_sum(): return value + lax.ppermute(value, axis, pairs)  35.3 us
    all_to_all x1, blocking collectives, per_device(): parts = lax.all_to_all(mine, 'dp_1', 0, 0, tiled=True)  30.7 us
    ppermute x9, starting transfers between devices, swap_sum(): return value + lax.ppermute(value, axis, pairs)  26.7 us
    all_to_all x1, starting transfers between devices, per_device(): arrived = lax.all_to_all(pieces, ('dp_0', 'grp'), 0, 0, tiled=True)  16.3 us
    pallas_call x1, Pallas kernels, run_steps(): pl.pallas_call(steps_kernel, out_shape=(half, half, jax.ShapeDtypeStruct(...  15.7 us
    all_to_all x1, waiting for transfers between devices, per_device(): whole = lax.all_to_all(copies, 'grp', 0, 0, tiled=True)  7.64 us
    ppermute x1, waiting for transfers between devices, per_device(): mine = keep + lax.ppermute(send, 'dp_2', [(0, 1), (1, 0)])  4.34 us
    all_to_all x1, starting transfers between devices, per_device(): whole = lax.all_to_all(copies, 'grp', 0, 0, tiled=True)  3.35 us
  transfers between devices with their start and end apart: 12, of which 10 were waited for; matrix products, arithmetic and copies ran while one was open for 1% of the time, Pallas kernels for 0%

profile of v1, /device:TPU:32, one launch (start us, length us, event | category | flops | bytes accessed | tf_op | source)
XLA Modules:
  0.0 147.6 jit_solution(8595468814114590295)
XLA Ops:
  0.6 15.7 %milstein_steps.1 = (f32[4,8,128,128]{3,2,1,0:T(8,128)}, f32[4,8,128,128]{3,2,1,0:T(8,128)}, f32[8,128]{1,0:T(8,128)}) custom-call(s32[1]{0:T(128)} %bitcast.core_ref, bf16[128,512]{1,0:T(8,128)(2,1)} %start_hbm.1, bf16[512,1024]{1,0:T(8,128)(2,1)} %w_up_hbm.1, f32[1,1024]{1,0:T(1,128)} %bitcast.12, bf16[1024,512]{1,0:T(8,128)(2,1)} %w_down_hbm.1, ...), custom_call_target="tpu_custom_call" | custom-call | tf_op jit(solution)/shard_map/milstein_steps/pallas_call | solution.py:189
  16.3 1.9 %collective-permute-start.9 = (f32[4,8,128,128]{3,2,1,0:T(8,128)}, f32[4,8,128,128]{3,2,1,0:T(8,128)S(1)}, u32[]{:S(2)}, u32[]{:S(2)}) collective-permute-start(f32[4,8,128,128]{3,2,1,0:T(8,128)} %get-tuple-element.8), channel_id=1, source_target_pairs={{0,1},{1,0},{2,3},{3,2},{4,5},{5,4},{6,7},{7,6},{8,9},{9,8},{10,11... | collective-permute-start | bytes 6291464 | tf_op jit(solution)/shard_map/ppermute | solution.py:243
  18.3 4.3 %collective-permute-done.9 = f32[4,8,128,128]{3,2,1,0:T(8,128)S(1)} collective-permute-done((f32[4,8,128,128]{3,2,1,0:T(8,128)}, f32[4,8,128,128]{3,2,1,0:T(8,128)S(1)}, u32[]{:S(2)}, u32[]{:S(2)}) %collective-permute-start.9) | collective-permute-done | bytes 2097184 | tf_op jit(solution)/shard_map/ppermute | solution.py:243
  22.6 1.9 %add.39 = f32[4,8,128,128]{3,2,1,0:T(8,128)S(1)} add(f32[4,8,128,128]{3,2,1,0:T(8,128)} %get-tuple-element.7, f32[4,8,128,128]{3,2,1,0:T(8,128)S(1)} %collective-permute-done.9) | non-fusion elementwise | flops 524288 | bytes 6291456 | tf_op jit(solution)/shard_map/add | solution.py:243
  24.5 30.7 %all_to_all.15 = f32[4,8,128,128]{3,2,1,0:T(8,128)S(1)} all-to-all(f32[4,8,128,128]{3,2,1,0:T(8,128)S(1)} %add.39), channel_id=1, replica_groups=mesh['grp'=8,'dp_0'=8,'dp_1'=4,'dp_2'=2] {'dp_1'}, dimensions={0} | all-to-all | bytes 4194304 | tf_op jit(solution)/shard_map/all_to_all | solution.py:244
  55.2 0.0 copy-start
  55.2 1.0 reduce_sum.18
  56.2 16.3 %all-to-all-start.1 = ((f32[64,16,128]{2,1,0:T(8,128)}), f32[64,16,128]{2,1,0:T(8,128)S(1)}, u32[]{:S(2)}, u32[]{:S(2)}) async-start(f32[64,16,128]{2,1,0:T(8,128)} %bitcast.3), calls=%async_computation.1 | async-start | bytes 1048576 | tf_op jit(solution)/shard_map/all_to_all | solution.py:247
  72.5 0.0 copy-done
  72.5 1.9 %collective-permute-start = (f32[8,128]{1,0:T(8,128)S(1)}, f32[8,128]{1,0:T(8,128)S(1)}, u32[]{:S(2)}, u32[]{:S(2)}) collective-permute-start(f32[8,128]{1,0:T(8,128)S(1)} %copy-done), channel_id=1, source_target_pairs={{0,1},{1,0},{2,3},{3,2},{4,5},{5,4},{6,7},{7,6},{8,9},{9,8},{10,11... | collective-permute-start | bytes 12296 | tf_op jit(solution)/shard_map/ppermute | solution.py:225
  74.5 1.1 collective-permute-done
  75.6 2.5 %collective-permute-start.1 = (f32[8,128]{1,0:T(8,128)S(1)}, f32[8,128]{1,0:T(8,128)S(1)}, u32[]{:S(2)}, u32[]{:S(2)}) collective-permute-start(f32[8,128]{1,0:T(8,128)S(1)} %add.30), channel_id=1, source_target_pairs={{0,2},{2,4},{4,6},{6,0},{1,3},{3,5},{5,7},{7,1},{8,10},{10,12},{12... | collective-permute-start | bytes 12296 | tf_op jit(solution)/shard_map/ppermute | solution.py:225
  78.1 4.2 %collective-permute-done.1 = f32[8,128]{1,0:T(8,128)S(1)} collective-permute-done((f32[8,128]{1,0:T(8,128)S(1)}, f32[8,128]{1,0:T(8,128)S(1)}, u32[]{:S(2)}, u32[]{:S(2)}) %collective-permute-start.1) | collective-permute-done | bytes 4128 | tf_op jit(solution)/shard_map/ppermute | solution.py:225
  82.3 1.9 %collective-permute-start.2 = (f32[8,128]{1,0:T(8,128)S(1)}, f32[8,128]{1,0:T(8,128)S(1)}, u32[]{:S(2)}, u32[]{:S(2)}) collective-permute-start(f32[8,128]{1,0:T(8,128)S(1)} %add.31), channel_id=1, source_target_pairs={{0,4},{2,6},{4,0},{6,2},{1,5},{3,7},{5,1},{7,3},{8,12},{10,14},{12... | collective-permute-start | bytes 12296 | tf_op jit(solution)/shard_map/ppermute | solution.py:225
  84.2 5.1 %collective-permute-done.2 = f32[8,128]{1,0:T(8,128)S(1)} collective-permute-done((f32[8,128]{1,0:T(8,128)S(1)}, f32[8,128]{1,0:T(8,128)S(1)}, u32[]{:S(2)}, u32[]{:S(2)}) %collective-permute-start.2) | collective-permute-done | bytes 4128 | tf_op jit(solution)/shard_map/ppermute | solution.py:225
  89.3 2.5 %collective-permute-start.3 = (f32[8,128]{1,0:T(8,128)S(1)}, f32[8,128]{1,0:T(8,128)S(1)}, u32[]{:S(2)}, u32[]{:S(2)}) collective-permute-start(f32[8,128]{1,0:T(8,128)S(1)} %add.32), channel_id=1, source_target_pairs={{0,8},{8,16},{16,24},{24,32},{32,40},{40,48},{48,56},{56,0},{1,9},... | collective-permute-start | bytes 12296 | tf_op jit(solution)/shard_map/ppermute | solution.py:225
  91.8 4.2 %collective-permute-done.3 = f32[8,128]{1,0:T(8,128)S(1)} collective-permute-done((f32[8,128]{1,0:T(8,128)S(1)}, f32[8,128]{1,0:T(8,128)S(1)}, u32[]{:S(2)}, u32[]{:S(2)}) %collective-permute-start.3) | collective-permute-done | bytes 4128 | tf_op jit(solution)/shard_map/ppermute | solution.py:225
  96.0 1.9 %collective-permute-start.4 = (f32[8,128]{1,0:T(8,128)S(1)}, f32[8,128]{1,0:T(8,128)S(1)}, u32[]{:S(2)}, u32[]{:S(2)}) collective-permute-start(f32[8,128]{1,0:T(8,128)S(1)} %add.33), channel_id=1, source_target_pairs={{0,16},{8,24},{16,32},{24,40},{32,48},{40,56},{48,0},{56,8},{1,17}... | collective-permute-start | bytes 12296 | tf_op jit(solution)/shard_map/ppermute | solution.py:225
  97.9 5.7 %collective-permute-done.4 = f32[8,128]{1,0:T(8,128)S(1)} collective-permute-done((f32[8,128]{1,0:T(8,128)S(1)}, f32[8,128]{1,0:T(8,128)S(1)}, u32[]{:S(2)}, u32[]{:S(2)}) %collective-permute-start.4) | collective-permute-done | bytes 4128 | tf_op jit(solution)/shard_map/ppermute | solution.py:225
  103.6 2.3 %collective-permute-start.5 = (f32[8,128]{1,0:T(8,128)S(1)}, f32[8,128]{1,0:T(8,128)S(1)}, u32[]{:S(2)}, u32[]{:S(2)}) collective-permute-start(f32[8,128]{1,0:T(8,128)S(1)} %add.34), channel_id=1, source_target_pairs={{0,32},{8,40},{16,48},{24,56},{32,0},{40,8},{48,16},{56,24},{1,33}... | collective-permute-start | bytes 12296 | tf_op jit(solution)/shard_map/ppermute | solution.py:225
  105.9 7.1 %collective-permute-done.5 = f32[8,128]{1,0:T(8,128)S(1)} collective-permute-done((f32[8,128]{1,0:T(8,128)S(1)}, f32[8,128]{1,0:T(8,128)S(1)}, u32[]{:S(2)}, u32[]{:S(2)}) %collective-permute-start.5) | collective-permute-done | bytes 4128 | tf_op jit(solution)/shard_map/ppermute | solution.py:225
  113.0 3.4 %collective-permute-start.6 = (f32[8,128]{1,0:T(8,128)S(1)}, f32[8,128]{1,0:T(8,128)S(1)}, u32[]{:S(2)}, u32[]{:S(2)}) collective-permute-start(f32[8,128]{1,0:T(8,128)S(1)} %add.35), channel_id=1, source_target_pairs={{0,64},{64,128},{128,192},{192,256},{256,320},{320,384},{384,448},... | collective-permute-start | bytes 12296 | tf_op jit(solution)/shard_map/ppermute | solution.py:225
  116.4 3.3 %collective-permute-done.6 = f32[8,128]{1,0:T(8,128)S(1)} collective-permute-done((f32[8,128]{1,0:T(8,128)S(1)}, f32[8,128]{1,0:T(8,128)S(1)}, u32[]{:S(2)}, u32[]{:S(2)}) %collective-permute-start.6) | collective-permute-done | bytes 4128 | tf_op jit(solution)/shard_map/ppermute | solution.py:225
  119.7 3.1 %collective-permute-start.7 = (f32[8,128]{1,0:T(8,128)S(1)}, f32[8,128]{1,0:T(8,128)S(1)}, u32[]{:S(2)}, u32[]{:S(2)}) collective-permute-start(f32[8,128]{1,0:T(8,128)S(1)} %add.36), channel_id=1, source_target_pairs={{0,128},{64,192},{128,256},{192,320},{256,384},{320,448},{384,0},{... | collective-permute-start | bytes 12296 | tf_op jit(solution)/shard_map/ppermute | solution.py:225
  122.8 4.5 %collective-permute-done.7 = f32[8,128]{1,0:T(8,128)S(1)} collective-permute-done((f32[8,128]{1,0:T(8,128)S(1)}, f32[8,128]{1,0:T(8,128)S(1)}, u32[]{:S(2)}, u32[]{:S(2)}) %collective-permute-start.7) | collective-permute-done | bytes 4128 | tf_op jit(solution)/shard_map/ppermute | solution.py:225
  127.3 7.3 %collective-permute-start.8 = (f32[8,128]{1,0:T(8,128)S(1)}, f32[8,128]{1,0:T(8,128)S(1)}, u32[]{:S(2)}, u32[]{:S(2)}) collective-permute-start(f32[8,128]{1,0:T(8,128)S(1)} %add.37), channel_id=1, source_target_pairs={{0,256},{64,320},{128,384},{192,448},{256,0},{320,64},{384,128},{4... | collective-permute-start | bytes 12296 | tf_op jit(solution)/shard_map/ppermute | solution.py:225
  134.6 0.0 all-to-all-done.1
  134.6 0.1 reduce_sum.19
  134.7 0.6 broadcast_in_dim.15
  135.3 3.3 %all-to-all-start.2 = ((f32[8,16,128]{2,1,0:T(8,128)}), f32[8,16,128]{2,1,0:T(8,128)S(1)}, u32[]{:S(2)}, u32[]{:S(2)}) async-start(f32[8,16,128]{2,1,0:T(8,128)} %broadcast_in_dim.15), calls=%async_computation.2 | async-start | bytes 131072 | tf_op jit(solution)/shard_map/all_to_all | solution.py:250
  138.7 0.0 collective-permute-done.8
  138.7 0.6 sqrt_reduce_fusion
  139.4 7.6 %all-to-all-done.2 = f32[8,16,128]{2,1,0:T(8,128)S(1)} async-done(((f32[8,16,128]{2,1,0:T(8,128)}), f32[8,16,128]{2,1,0:T(8,128)S(1)}, u32[]{:S(2)}, u32[]{:S(2)}) %all-to-all-start.2) | async-done | bytes 65568 | tf_op jit(solution)/shard_map/all_to_all | solution.py:250
  147.0 0.6 slice_bitcast_fusion
  (9 shorter events, 0.0 us)
Async XLA Ops:
  16.3 6.3 %collective-permute-start.9 = (f32[4,8,128,128]{3,2,1,0:T(8,128)}, f32[4,8,128,128]{3,2,1,0:T(8,128)S(1)}, u32[]{:S(2)}, u32[]{:S(2)}) collective-permute-start(f32[4,8,128,128]{3,2,1,0:T(8,128)} %get-tuple-element.8), channel_id=1, source_target_pairs={{0,1},{1,0},{2,3},{3,2},{4,5},{5,4},{6,7},{7,6},{8,9},{9,8},{10,11... | collective-permute-start | bytes 6291464 | tf_op jit(solution)/shard_map/ppermute | solution.py:243
  55.2 17.3 %copy-start = (f32[8,128]{1,0:T(8,128)S(1)}, f32[8,128]{1,0:T(8,128)}, u32[]{:S(2)}) copy-start(f32[8,128]{1,0:T(8,128)} %get-tuple-element.6) | copy-start | bytes 12292
  56.2 78.5 %all-to-all-start.1 = ((f32[64,16,128]{2,1,0:T(8,128)}), f32[64,16,128]{2,1,0:T(8,128)S(1)}, u32[]{:S(2)}, u32[]{:S(2)}) async-start(f32[64,16,128]{2,1,0:T(8,128)} %bitcast.3), calls=%async_computation.1 | async-start | bytes 1048576 | tf_op jit(solution)/shard_map/all_to_all | solution.py:247
  72.5 3.1 %collective-permute-start = (f32[8,128]{1,0:T(8,128)S(1)}, f32[8,128]{1,0:T(8,128)S(1)}, u32[]{:S(2)}, u32[]{:S(2)}) collective-permute-start(f32[8,128]{1,0:T(8,128)S(1)} %copy-done), channel_id=1, source_target_pairs={{0,1},{1,0},{2,3},{3,2},{4,5},{5,4},{6,7},{7,6},{8,9},{9,8},{10,11... | collective-permute-start | bytes 12296 | tf_op jit(solution)/shard_map/ppermute | solution.py:225
  75.6 6.7 %collective-permute-start.1 = (f32[8,128]{1,0:T(8,128)S(1)}, f32[8,128]{1,0:T(8,128)S(1)}, u32[]{:S(2)}, u32[]{:S(2)}) collective-permute-start(f32[8,128]{1,0:T(8,128)S(1)} %add.30), channel_id=1, source_target_pairs={{0,2},{2,4},{4,6},{6,0},{1,3},{3,5},{5,7},{7,1},{8,10},{10,12},{12... | collective-permute-start | bytes 12296 | tf_op jit(solution)/shard_map/ppermute | solution.py:225
  82.3 7.0 %collective-permute-start.2 = (f32[8,128]{1,0:T(8,128)S(1)}, f32[8,128]{1,0:T(8,128)S(1)}, u32[]{:S(2)}, u32[]{:S(2)}) collective-permute-start(f32[8,128]{1,0:T(8,128)S(1)} %add.31), channel_id=1, source_target_pairs={{0,4},{2,6},{4,0},{6,2},{1,5},{3,7},{5,1},{7,3},{8,12},{10,14},{12... | collective-permute-start | bytes 12296 | tf_op jit(solution)/shard_map/ppermute | solution.py:225
  89.3 6.7 %collective-permute-start.3 = (f32[8,128]{1,0:T(8,128)S(1)}, f32[8,128]{1,0:T(8,128)S(1)}, u32[]{:S(2)}, u32[]{:S(2)}) collective-permute-start(f32[8,128]{1,0:T(8,128)S(1)} %add.32), channel_id=1, source_target_pairs={{0,8},{8,16},{16,24},{24,32},{32,40},{40,48},{48,56},{56,0},{1,9},... | collective-permute-start | bytes 12296 | tf_op jit(solution)/shard_map/ppermute | solution.py:225
  96.0 7.6 %collective-permute-start.4 = (f32[8,128]{1,0:T(8,128)S(1)}, f32[8,128]{1,0:T(8,128)S(1)}, u32[]{:S(2)}, u32[]{:S(2)}) collective-permute-start(f32[8,128]{1,0:T(8,128)S(1)} %add.33), channel_id=1, source_target_pairs={{0,16},{8,24},{16,32},{24,40},{32,48},{40,56},{48,0},{56,8},{1,17}... | collective-permute-start | bytes 12296 | tf_op jit(solution)/shard_map/ppermute | solution.py:225
  103.6 9.4 %collective-permute-start.5 = (f32[8,128]{1,0:T(8,128)S(1)}, f32[8,128]{1,0:T(8,128)S(1)}, u32[]{:S(2)}, u32[]{:S(2)}) collective-permute-start(f32[8,128]{1,0:T(8,128)S(1)} %add.34), channel_id=1, source_target_pairs={{0,32},{8,40},{16,48},{24,56},{32,0},{40,8},{48,16},{56,24},{1,33}... | collective-permute-start | bytes 12296 | tf_op jit(solution)/shard_map/ppermute | solution.py:225
  113.0 6.7 %collective-permute-start.6 = (f32[8,128]{1,0:T(8,128)S(1)}, f32[8,128]{1,0:T(8,128)S(1)}, u32[]{:S(2)}, u32[]{:S(2)}) collective-permute-start(f32[8,128]{1,0:T(8,128)S(1)} %add.35), channel_id=1, source_target_pairs={{0,64},{64,128},{128,192},{192,256},{256,320},{320,384},{384,448},... | collective-permute-start | bytes 12296 | tf_op jit(solution)/shard_map/ppermute | solution.py:225
  119.7 7.6 %collective-permute-start.7 = (f32[8,128]{1,0:T(8,128)S(1)}, f32[8,128]{1,0:T(8,128)S(1)}, u32[]{:S(2)}, u32[]{:S(2)}) collective-permute-start(f32[8,128]{1,0:T(8,128)S(1)} %add.36), channel_id=1, source_target_pairs={{0,128},{64,192},{128,256},{192,320},{256,384},{320,448},{384,0},{... | collective-permute-start | bytes 12296 | tf_op jit(solution)/shard_map/ppermute | solution.py:225
  127.3 11.4 %collective-permute-start.8 = (f32[8,128]{1,0:T(8,128)S(1)}, f32[8,128]{1,0:T(8,128)S(1)}, u32[]{:S(2)}, u32[]{:S(2)}) collective-permute-start(f32[8,128]{1,0:T(8,128)S(1)} %add.37), channel_id=1, source_target_pairs={{0,256},{64,320},{128,384},{192,448},{256,0},{320,64},{384,128},{4... | collective-permute-start | bytes 12296 | tf_op jit(solution)/shard_map/ppermute | solution.py:225
  135.3 11.7 %all-to-all-start.2 = ((f32[8,16,128]{2,1,0:T(8,128)}), f32[8,16,128]{2,1,0:T(8,128)S(1)}, u32[]{:S(2)}, u32[]{:S(2)}) async-start(f32[8,16,128]{2,1,0:T(8,128)} %broadcast_in_dim.15), calls=%async_computation.2 | async-start | bytes 131072 | tf_op jit(solution)/shard_map/all_to_all | solution.py:250

commit v2 on v1

v2 whole, which is shorter than its diff:
```python
import jax
import jax.numpy as jnp
from jax import lax
from jax.experimental import pallas as pl
from jax.experimental.pallas import tpu as pltpu
from jax.sharding import Mesh
from jax.sharding import PartitionSpec as P

GRP = ("z_far", "z_mid", "z_pair")
DP = ("y_far", "y_pair", "x", "core")
GRP_DP = GRP + DP

base_step = 0.05
abs_tol = 0.01
rel_tol = 0.01
F32 = jnp.float32
BF16 = jnp.bfloat16
X = 4
PAIR = 2


def mm(a, b):
    return jnp.dot(a, b, preferred_element_type=F32)


def mm_t(a, b):
    return lax.dot_general(a, b, (((1,), (1,)), ((), ())), preferred_element_type=F32)


def t_mm(a, b):
    return lax.dot_general(a, b, (((0,), (0,)), ((), ())), preferred_element_type=F32)


def sigmoid(x):
    return 0.5 * jnp.tanh(0.5 * x) + 0.5


def steps_kernel(
    core_ref,
    start_hbm, w_up_hbm, b_up_hbm, w_down_hbm, w_spread_hbm, w_scale_hbm, b_scale_hbm,
    noise_hbm, mults_hbm, flags_hbm, cot_hbm,
    keep_ref, send_ref,
    start_v, w_up, b_up_v, w_down, w_spread, w_scale, b_scale_v, noise_v, mults_v, flags_v, cot_v,
    d_pre, d_one, d_two, hid_v, low_v, cpre_v, cdrift_v, d_g, d_gbar, fac_v, dw_v,
    in_sems,
):
    steps, rows, latent = noise_v.shape
    loads = {}
    for slot, (name, src, dst) in enumerate((
        ("start", start_hbm, start_v),
        ("mults", mults_hbm, mults_v),
        ("flags", flags_hbm, flags_v),
        ("b_up", b_up_hbm, b_up_v),
        ("b_scale", b_scale_hbm, b_scale_v),
        ("spread", w_spread_hbm, w_spread),
        ("scale", w_scale_hbm, w_scale),
        ("up", w_up_hbm, w_up),
        ("noise", noise_hbm, noise_v),
        ("down", w_down_hbm, w_down),
        ("cot", cot_hbm, cot_v),
    )):
        loads[name] = pltpu.make_async_copy(src, dst, in_sems.at[slot])
        loads[name].start()

    def need(*names):
        for name in names:
            if name in loads:
                loads.pop(name).wait()

    need("start", "mults", "flags", "b_up", "b_scale")
    per_row = jnp.concatenate(
        [
            mults_v[...].astype(F32) * base_step,
            flags_v[...].astype(F32),
            jnp.zeros((8 - 2 * steps, rows), F32),
        ],
        axis=0,
    )
    columns = jnp.transpose(per_row)
    b_up = b_up_v[...]
    b_scale = b_scale_v[...]
    state = start_v[...].astype(F32)

    def gated(pre):
        sig = sigmoid(pre)
        return (pre * sig).astype(BF16), sig * (1.0 + pre * (1.0 - sig))

    err_parts = []
    for n in range(steps):
        h = columns[:, n : n + 1]
        keep = columns[:, steps + n : steps + n + 1]
        root = jnp.sqrt(h)
        low = state.astype(BF16)
        low_v[n * rows : (n + 1) * rows, :] = low
        need("spread")
        inner, slope = gated(mm(low, w_spread[...]))
        d_one[n] = slope
        need("scale")
        sig_g = sigmoid(mm(inner, w_scale[...]) + b_scale)
        spread = 0.6 * sig_g
        d_g[n] = spread * (1.0 - sig_g)
        shifted_low = (state + spread * root).astype(BF16)
        inner, slope = gated(mm(shifted_low, w_spread[...]))
        d_two[n] = slope
        sig_s = sigmoid(mm(inner, w_scale[...]) + b_scale)
        shifted = 0.6 * sig_s
        d_gbar[n] = shifted * (1.0 - sig_s)
        need("up")
        hidden, slope = gated(mm(low, w_up[...]) + b_up)
        hid_v[n * rows : (n + 1) * rows, :] = hidden
        d_pre[n] = slope
        need("noise")
        brownian = root * noise_v[n].astype(F32)
        factor = (brownian * brownian - h) / (2.0 * root)
        dw_v[n] = brownian
        fac_v[n] = factor
        milstein = (shifted - spread) * factor
        scaled = milstein / (abs_tol + rel_tol * jnp.abs(state))
        err_parts.append(jnp.sum((scaled * scaled).reshape(rows // 8, 8, latent), axis=0))
        if n + 1 < steps:
            need("down")
            drift = mm(hidden, w_down[...])
            proposal = state + drift * h + spread * brownian + milstein
            state = keep * proposal + (1.0 - keep) * state

    err_rows = [jnp.sum(jnp.sum(p, axis=0, keepdims=True), axis=1, keepdims=True) for p in err_parts]
    row = lax.broadcasted_iota(jnp.int32, (8, 128), 0)
    err = jnp.zeros((8, 128), F32)
    for n in range(steps):
        err = jnp.where(row == n, err_rows[n], err)

    need("down")
    need("cot")
    cot = cot_v[...].astype(F32)

    def through_net(d_out, slope):
        d_inner = mm_t(d_out.astype(BF16), w_scale[...]).astype(BF16).astype(F32)
        return mm_t((d_inner * slope).astype(BF16), w_spread[...]).astype(BF16).astype(F32)

    for n in reversed(range(steps)):
        h = columns[:, n : n + 1]
        keep = columns[:, steps + n : steps + n + 1]
        root = jnp.sqrt(h)
        kept = cot * keep
        cdrift = (kept * h).astype(BF16)
        cdrift_v[n * rows : (n + 1) * rows, :] = cdrift
        cpre = (mm_t(cdrift, w_down[...]) * d_pre[n]).astype(BF16)
        cpre_v[n * rows : (n + 1) * rows, :] = cpre
        if n > 0:
            d_shift = kept * fac_v[n]
            d_state = through_net(d_shift * d_gbar[n], d_two[n])
            d_spread = kept * dw_v[n] - d_shift + d_state * root
            d_first = through_net(d_spread * d_g[n], d_one[n])
            cot = (kept + (1.0 - keep) * cot) + d_state + d_first + mm_t(cpre, w_up[...])

    tiles = w_up.shape[1] // 128
    sums = keep_ref.shape[1] - 8
    first = core_ref[0] == 0

    def place(grad, which):
        for q in range(latent // 16):
            far, pair, x = q // (PAIR * X), q // X % PAIR, q % X
            part = (x * PAIR + pair) * 2 + which
            for t in range(tiles):
                even = grad[16 * q : 16 * q + 8, t * 128 : (t + 1) * 128]
                odd = grad[16 * q + 8 : 16 * q + 16, t * 128 : (t + 1) * 128]
                at = (far * tiles + t) * 8
                keep_ref[part, at : at + 8, :] = jnp.where(first, even, odd)
                send_ref[part, at : at + 8, :] = jnp.where(first, odd, even)

    for part in range(keep_ref.shape[0]):
        keep_ref[part, sums : sums + 8, :] = err
        send_ref[part, sums : sums + 8, :] = err
    place(t_mm(cdrift_v[...], hid_v[...]), 1)
    place(t_mm(low_v[...], cpre_v[...]), 0)


def run_steps(core, *args):
    start, w_up, _, _, _, _, _, noise, _, _, _ = args
    steps, rows, latent = noise.shape
    wide = w_up.shape[1]
    parts = X * PAIR * 2
    hbm = pl.BlockSpec(memory_space=pltpu.HBM)
    vmem = pl.BlockSpec(memory_space=pltpu.VMEM)
    smem = pl.BlockSpec(memory_space=pltpu.SMEM)
    half = pltpu.VMEM((parts, latent * wide // (parts * 128) + 8, 128), F32)
    return pl.pallas_call(
        steps_kernel,
        out_shape=(half, half),
        in_specs=[smem] + [hbm] * len(args),
        out_specs=(vmem, vmem),
        scratch_shapes=[
            *(pltpu.VMEM(a.shape, a.dtype) for a in args),
            pltpu.VMEM((steps, rows, wide), F32),
            pltpu.VMEM((steps, rows, wide), F32),
            pltpu.VMEM((steps, rows, wide), F32),
            pltpu.VMEM((steps * rows, wide), BF16),
            pltpu.VMEM((steps * rows, latent), BF16),
            pltpu.VMEM((steps * rows, wide), BF16),
            pltpu.VMEM((steps * rows, latent), BF16),
            pltpu.VMEM((steps, rows, latent), F32),
            pltpu.VMEM((steps, rows, latent), F32),
            pltpu.VMEM((steps, rows, latent), F32),
            pltpu.VMEM((steps, rows, latent), F32),
            pltpu.SemaphoreType.DMA((len(args),)),
        ],
        compiler_params=pltpu.CompilerParams(vmem_limit_bytes=32 * 1024 * 1024),
        name="milstein_steps",
    )(core, *(pltpu.with_memory_space_constraint(a, pltpu.HBM) for a in args))


def summed(parts, axes):
    return jnp.sum(lax.all_to_all(parts, axes, 0, 0, tiled=True), axis=0)


def per_device(
    start_state, w_up, b_up, w_down, w_spread, w_scale, b_scale,
    brownian_noise, step_mults, accept_flags, cotangent,
):
    groups = lax.axis_size(GRP)
    members = lax.axis_size(DP)
    row_count = start_state.shape[0] * start_state.shape[1] * groups * members
    steps = brownian_noise.shape[0]
    wide = w_up.shape[1]
    core = lax.axis_index("core")[None]
    keep, send = run_steps(
        core, start_state, w_up, b_up[None], w_down, w_spread, w_scale, b_scale[None],
        brownian_noise, step_mults, accept_flags, cotangent,
    )
    mine = keep + lax.ppermute(send, "core", [(0, 1), (1, 0)])
    part = summed(mine, ("x", "y_pair", "z_pair"))
    far = lax.axis_size("y_far")
    sums, err = part[:-8].reshape(far, -1, 128), part[-8:]
    pieces = jnp.concatenate([sums, jnp.broadcast_to(err, (far, 8, 128))], axis=1)
    piece = summed(pieces, "y_far")
    copies = jnp.broadcast_to(piece, (groups, *piece.shape))
    arrived = lax.all_to_all(copies, GRP, 0, 0, tiled=True)
    whole = jnp.sum(arrived.reshape(groups // 2, 2, *piece.shape), axis=0)
    grads = whole[:, :-8].reshape(2, wide // 128, 8, 128).transpose(0, 2, 1, 3).reshape(2, 8, wide)
    err_norms = jnp.sqrt(whole[0, -8 : steps - 8, 0] / row_count)
    return (err_norms, grads[0], grads[1])


def solution(mesh):
    split = Mesh(mesh.devices.reshape(mesh.shape["grp"] // 4, 2, 2, -1, PAIR, X, 2), GRP_DP)
    return jax.shard_map(
        per_device,
        mesh=split,
        in_specs=(
            P(GRP_DP, None), P(), P(), P(), P(), P(), P(),
            P(None, GRP_DP, None), P(None, GRP_DP), P(None, GRP_DP), P(GRP_DP, None),
        ),
        out_specs=(P(), P(DP, None), P(DP, None)),
        check_vma=False,
    )
```

time: 148 us -> 91.4 us (0.62)
  the two profiles are of different devices: /device:TPU:32 before, /device:TPU:8 now
where the time goes in v2:
time: 91.4 us; the launch traced here: 91.2 us
  blocking collectives  70.2 us (77%)
  Pallas kernels  12.5 us (14%)
  waiting for transfers between devices  4.22 us (5%)
  starting transfers between devices  1.92 us (2%)
  other arithmetic  1 us (1%)
    all_to_all x2, blocking collectives, summed(): return jnp.sum(lax.all_to_all(parts, axes, 0, 0, tiled=True), axis=0)  50.1 us
    all_to_all x1, blocking collectives, per_device(): arrived = lax.all_to_all(copies, GRP, 0, 0, tiled=True)  20 us
    pallas_call x1, Pallas kernels, run_steps(): pl.pallas_call(steps_kernel, out_shape=(half, half), in_specs=[smem] + [h...  12.5 us
    ppermute x1, waiting for transfers between devices, per_device(): mine = keep + lax.ppermute(send, 'core', [(0, 1), (1, 0)])  4.22 us
    ppermute x1, starting transfers between devices, per_device(): mine = keep + lax.ppermute(send, 'core', [(0, 1), (1, 0)])  1.92 us
  transfers between devices with their start and end apart: 1, of which 1 were waited for; matrix products, arithmetic and copies ran while one was open for 0% of the time, Pallas kernels for 0%

profile of v2, /device:TPU:8, one launch (start us, length us, event | category | flops | bytes accessed | tf_op | source)
XLA Modules:
  0.0 91.2 jit_solution(8992129467274993138)
XLA Ops:
  0.6 12.5 %milstein_steps.1 = (f32[16,264,128]{2,1,0:T(8,128)S(1)}, f32[16,264,128]{2,1,0:T(8,128)S(1)}) custom-call(s32[1]{0:T(128)} %bitcast.core_ref, bf16[128,512]{1,0:T(8,128)(2,1)} %start_hbm.1, bf16[512,1024]{1,0:T(8,128)(2,1)} %w_up_hbm.1, f32[1,1024]{1,0:T(1,128)} %bitcast.15, bf16[1024,512]{1,0:T(8,128)(2,1)} %w_down_hbm.1, bf16[512,1024]{1,0:T(8,128)(2,1)} %w_spread_hbm.1, ...), custom_call_target="tpu_custom_call" | custom-call | tf_op jit(solution)/shard_map/milstein_steps/pallas_call | solution.py:187
  13.1 1.9 %collective-permute-start = (f32[16,264,128]{2,1,0:T(8,128)S(1)}, f32[16,264,128]{2,1,0:T(8,128)S(1)}, u32[]{:S(2)}, u32[]{:S(2)}) collective-permute-start(f32[16,264,128]{2,1,0:T(8,128)S(1)} %get-tuple-element.6), channel_id=1, source_target_pairs={{0,1},{1,0},{2,3},{3,2},{4,5},{5,4},{6,7},{7,6},{8,9},{9,8},{10,11... | collective-permute-start | bytes 6488072 | tf_op jit(solution)/shard_map/ppermute | solution.py:230
  15.0 4.2 %collective-permute-done = f32[16,264,128]{2,1,0:T(8,128)S(1)} collective-permute-done((f32[16,264,128]{2,1,0:T(8,128)S(1)}, f32[16,264,128]{2,1,0:T(8,128)S(1)}, u32[]{:S(2)}, u32[]{:S(2)}) %collective-permute-start) | collective-permute-done | bytes 2162720 | tf_op jit(solution)/shard_map/ppermute | solution.py:230
  19.2 0.2 add.3
  19.5 36.3 %all_to_all.15 = f32[16,264,128]{2,1,0:T(8,128)S(1)} all-to-all(f32[16,264,128]{2,1,0:T(8,128)S(1)} %add.3), channel_id=1, replica_groups=mesh['z_far'=2,'z_mid'=2,'z_pair'=2,'y_far'=4,'y_pair'=2,'x'=4,'core'=2]..., dimensions={0} | all-to-all | bytes 4325376 | tf_op jit(solution)/shard_map/all_to_all | solution.py:213
  55.8 0.1 reduce_sum.27
  56.0 13.8 %all_to_all.16 = f32[4,72,128]{2,1,0:T(8,128)S(1)} all-to-all(f32[4,72,128]{2,1,0:T(8,128)S(1)} %pad_maximum_fusion), channel_id=1, replica_groups=mesh['z_far'=2,'z_mid'=2,'z_pair'=2,'y_far'=4,'y_pair'=2,'x'=4,'core'=2]..., dimensions={0} | all-to-all | bytes 294912 | tf_op jit(solution)/shard_map/all_to_all | solution.py:213
  69.8 20.0 %all_to_all.17 = f32[8,72,128]{2,1,0:T(8,128)S(1)} all-to-all(f32[8,72,128]{2,1,0:T(8,128)S(1)} %broadcast_in_dim.19), channel_id=1, replica_groups=mesh['z_far'=2,'z_mid'=2,'z_pair'=2,'y_far'=4,'y_pair'=2,'x'=4,'core'=2]..., dimensions={0} | all-to-all | bytes 589824 | tf_op jit(solution)/shard_map/all_to_all | solution.py:237
  89.9 0.6 fusion.1
  90.5 0.6 slice_bitcast_fusion.1
  (8 shorter events, 0.1 us)
Async XLA Ops:
  13.1 6.1 %collective-permute-start = (f32[16,264,128]{2,1,0:T(8,128)S(1)}, f32[16,264,128]{2,1,0:T(8,128)S(1)}, u32[]{:S(2)}, u32[]{:S(2)}) collective-permute-start(f32[16,264,128]{2,1,0:T(8,128)S(1)} %get-tuple-element.6), channel_id=1, source_target_pairs={{0,1},{1,0},{2,3},{3,2},{4,5},{5,4},{6,7},{7,6},{8,9},{9,8},{10,11... | collective-permute-start | bytes 6488072 | tf_op jit(solution)/shard_map/ppermute | solution.py:230

commit v3 on v2

--- a/solution.py
+++ b/solution.py
@@ -42,6 +42,7 @@
     keep_ref, send_ref,
     start_v, w_up, b_up_v, w_down, w_spread, w_scale, b_scale_v, noise_v, mults_v, flags_v, cot_v,
     d_pre, d_one, d_two, hid_v, low_v, cpre_v, cdrift_v, d_g, d_gbar, fac_v, dw_v,
+    wt_down, wt_up, wt_scale, wt_spread,
     in_sems,
 ):
     steps, rows, latent = noise_v.shape
@@ -122,6 +123,11 @@
             drift = mm(hidden, w_down[...])
             proposal = state + drift * h + spread * brownian + milstein
             state = keep * proposal + (1.0 - keep) * state
+            if n == 1:
+                wt_down[...] = jnp.transpose(w_down[...])
+                wt_scale[...] = jnp.transpose(w_scale[...])
+                wt_spread[...] = jnp.transpose(w_spread[...])
+                wt_up[...] = jnp.transpose(w_up[...])
 
     err_rows = [jnp.sum(jnp.sum(p, axis=0, keepdims=True), axis=1, keepdims=True) for p in err_parts]
     row = lax.broadcasted_iota(jnp.int32, (8, 128), 0)
@@ -134,8 +140,8 @@
     cot = cot_v[...].astype(F32)
 
     def through_net(d_out, slope):
-        d_inner = mm_t(d_out.astype(BF16), w_scale[...]).astype(BF16).astype(F32)
-        return mm_t((d_inner * slope).astype(BF16), w_spread[...]).astype(BF16).astype(F32)
+        d_inner = mm(d_out.astype(BF16), wt_scale[...]).astype(BF16).astype(F32)
+        return mm((d_inner * slope).astype(BF16), wt_spread[...]).astype(BF16).astype(F32)
 
     for n in reversed(range(steps)):
         h = columns[:, n : n + 1]
@@ -144,14 +150,14 @@
         kept = cot * keep
         cdrift = (kept * h).astype(BF16)
         cdrift_v[n * rows : (n + 1) * rows, :] = cdrift
-        cpre = (mm_t(cdrift, w_down[...]) * d_pre[n]).astype(BF16)
+        cpre = (mm(cdrift, wt_down[...]) * d_pre[n]).astype(BF16)
         cpre_v[n * rows : (n + 1) * rows, :] = cpre
         if n > 0:
             d_shift = kept * fac_v[n]
             d_state = through_net(d_shift * d_gbar[n], d_two[n])
             d_spread = kept * dw_v[n] - d_shift + d_state * root
             d_first = through_net(d_spread * d_g[n], d_one[n])
-            cot = (kept + (1.0 - keep) * cot) + d_state + d_first + mm_t(cpre, w_up[...])
+            cot = (kept + (1.0 - keep) * cot) + d_state + d_first + mm(cpre, wt_up[...])
 
     tiles = w_up.shape[1] // 128
     sums = keep_ref.shape[1] - 8
@@ -202,6 +208,10 @@
             pltpu.VMEM((steps, rows, latent), F32),
             pltpu.VMEM((steps, rows, latent), F32),
             pltpu.VMEM((steps, rows, latent), F32),
+            pltpu.VMEM((latent, wide), BF16),
+            pltpu.VMEM((wide, latent), BF16),
+            pltpu.VMEM((latent, wide), BF16),
+            pltpu.VMEM((wide, latent), BF16),
             pltpu.SemaphoreType.DMA((len(args),)),
         ],
         compiler_params=pltpu.CompilerParams(vmem_limit_bytes=32 * 1024 * 1024),

time: 91.4 us -> 89.3 us (0.977)
  Pallas kernels: 12.5 us -> 10.4 us
    pallas_call x1, Pallas kernels: 12.5 us -> 10.4 us  [run_steps(): pl.pallas_call(steps_kernel, out_shape=(half, half), in_specs=[smem] + [h...]
where the time goes in v3:
time: 89.3 us; the launch traced here: 89.1 us
  blocking collectives  70.2 us (79%)
  Pallas kernels  10.4 us (12%)
  waiting for transfers between devices  4.22 us (5%)
  starting transfers between devices  1.92 us (2%)
  other arithmetic  1 us (1%)
    all_to_all x2, blocking collectives, summed(): return jnp.sum(lax.all_to_all(parts, axes, 0, 0, tiled=True), axis=0)  50.1 us
    all_to_all x1, blocking collectives, per_device(): arrived = lax.all_to_all(copies, GRP, 0, 0, tiled=True)  20 us
    pallas_call x1, Pallas kernels, run_steps(): pl.pallas_call(steps_kernel, out_shape=(half, half), in_specs=[smem] + [h...  10.4 us
    ppermute x1, waiting for transfers between devices, per_device(): mine = keep + lax.ppermute(send, 'core', [(0, 1), (1, 0)])  4.22 us
    ppermute x1, starting transfers between devices, per_device(): mine = keep + lax.ppermute(send, 'core', [(0, 1), (1, 0)])  1.92 us
  transfers between devices with their start and end apart: 1, of which 1 were waited for; matrix products, arithmetic and copies ran while one was open for 0% of the time, Pallas kernels for 0%

profile of v3, /device:TPU:8, one launch (start us, length us, event | category | flops | bytes accessed | tf_op | source)
XLA Modules:
  0.0 89.1 jit_solution(5181070421787658695)
XLA Ops:
  0.6 10.4 %milstein_steps.1 = (f32[16,264,128]{2,1,0:T(8,128)S(1)}, f32[16,264,128]{2,1,0:T(8,128)S(1)}) custom-call(s32[1]{0:T(128)} %bitcast.core_ref, bf16[128,512]{1,0:T(8,128)(2,1)} %start_hbm.1, bf16[512,1024]{1,0:T(8,128)(2,1)} %w_up_hbm.1, f32[1,1024]{1,0:T(1,128)} %bitcast.15, bf16[1024,512]{1,0:T(8,128)(2,1)} %w_down_hbm.1, bf16[512,1024]{1,0:T(8,128)(2,1)} %w_spread_hbm.1, ...), custom_call_target="tpu_custom_call" | custom-call | tf_op jit(solution)/shard_map/milstein_steps/pallas_call | solution.py:193
  11.0 1.9 %collective-permute-start = (f32[16,264,128]{2,1,0:T(8,128)S(1)}, f32[16,264,128]{2,1,0:T(8,128)S(1)}, u32[]{:S(2)}, u32[]{:S(2)}) collective-permute-start(f32[16,264,128]{2,1,0:T(8,128)S(1)} %get-tuple-element.6), channel_id=1, source_target_pairs={{0,1},{1,0},{2,3},{3,2},{4,5},{5,4},{6,7},{7,6},{8,9},{9,8},{10,11... | collective-permute-start | bytes 6488072 | tf_op jit(solution)/shard_map/ppermute | solution.py:240
  13.0 4.2 %collective-permute-done = f32[16,264,128]{2,1,0:T(8,128)S(1)} collective-permute-done((f32[16,264,128]{2,1,0:T(8,128)S(1)}, f32[16,264,128]{2,1,0:T(8,128)S(1)}, u32[]{:S(2)}, u32[]{:S(2)}) %collective-permute-start) | collective-permute-done | bytes 2162720 | tf_op jit(solution)/shard_map/ppermute | solution.py:240
  17.2 0.2 add.3
  17.4 36.3 %all_to_all.15 = f32[16,264,128]{2,1,0:T(8,128)S(1)} all-to-all(f32[16,264,128]{2,1,0:T(8,128)S(1)} %add.3), channel_id=1, replica_groups=mesh['z_far'=2,'z_mid'=2,'z_pair'=2,'y_far'=4,'y_pair'=2,'x'=4,'core'=2]..., dimensions={0} | all-to-all | bytes 4325376 | tf_op jit(solution)/shard_map/all_to_all | solution.py:223
  53.7 0.1 reduce_sum.27
  53.9 13.8 %all_to_all.16 = f32[4,72,128]{2,1,0:T(8,128)S(1)} all-to-all(f32[4,72,128]{2,1,0:T(8,128)S(1)} %pad_maximum_fusion), channel_id=1, replica_groups=mesh['z_far'=2,'z_mid'=2,'z_pair'=2,'y_far'=4,'y_pair'=2,'x'=4,'core'=2]..., dimensions={0} | all-to-all | bytes 294912 | tf_op jit(solution)/shard_map/all_to_all | solution.py:223
  67.8 20.0 %all_to_all.17 = f32[8,72,128]{2,1,0:T(8,128)S(1)} all-to-all(f32[8,72,128]{2,1,0:T(8,128)S(1)} %broadcast_in_dim.19), channel_id=1, replica_groups=mesh['z_far'=2,'z_mid'=2,'z_pair'=2,'y_far'=4,'y_pair'=2,'x'=4,'core'=2]..., dimensions={0} | all-to-all | bytes 589824 | tf_op jit(solution)/shard_map/all_to_all | solution.py:247
  87.8 0.6 fusion.1
  88.5 0.6 slice_bitcast_fusion.1
  (8 shorter events, 0.1 us)
Async XLA Ops:
  11.0 6.1 %collective-permute-start = (f32[16,264,128]{2,1,0:T(8,128)S(1)}, f32[16,264,128]{2,1,0:T(8,128)S(1)}, u32[]{:S(2)}, u32[]{:S(2)}) collective-permute-start(f32[16,264,128]{2,1,0:T(8,128)S(1)} %get-tuple-element.6), channel_id=1, source_target_pairs={{0,1},{1,0},{2,3},{3,2},{4,5},{5,4},{6,7},{7,6},{8,9},{9,8},{10,11... | collective-permute-start | bytes 6488072 | tf_op jit(solution)/shard_map/ppermute | solution.py:240

commit v4 on v3

--- a/solution.py
+++ b/solution.py
@@ -106,7 +106,7 @@
         sig_s = sigmoid(mm(inner, w_scale[...]) + b_scale)
         shifted = 0.6 * sig_s
         d_gbar[n] = shifted * (1.0 - sig_s)
-        need("up")
+        need("up", "noise", "down", "cot")
         hidden, slope = gated(mm(low, w_up[...]) + b_up)
         hid_v[n * rows : (n + 1) * rows, :] = hidden
         d_pre[n] = slope
@@ -219,6 +219,38 @@
     )(core, *(pltpu.with_memory_space_constraint(a, pltpu.HBM) for a in args))
 
 
+def finish(arrived, steps, wide, row_count):
+    tiles = wide // 128
+    sums = tiles * 8
+
+    def kernel(arrived_ref, err_ref, up_ref, down_ref):
+        def total(which, start, size):
+            pieces = [arrived_ref[k, start : start + size, :] for k in range(which, arrived_ref.shape[0], 2)]
+            while len(pieces) > 1:
+                pieces = [a + b for a, b in zip(pieces[::2], pieces[1::2])]
+            return pieces[0]
+
+        for which, out in ((0, up_ref), (1, down_ref)):
+            for t in range(tiles):
+                out[:, t * 128 : (t + 1) * 128] = total(which, t * 8, 8)
+        err = total(0, sums, 8)
+        row = lax.broadcasted_iota(jnp.int32, err.shape, 0)
+        lane = lax.broadcasted_iota(jnp.int32, err.shape, 1)
+        norms = jnp.sqrt(jnp.sum(jnp.where(row == lane, err, 0.0), axis=0) / row_count)
+        err_ref[...] = norms[:steps]
+
+    vmem = pl.BlockSpec(memory_space=pltpu.VMEM)
+    grad = jax.ShapeDtypeStruct((8, wide), F32)
+    return pl.pallas_call(
+        kernel,
+        out_shape=(jax.ShapeDtypeStruct((steps,), F32), grad, grad),
+        in_specs=[vmem],
+        out_specs=(vmem, vmem, vmem),
+        compiler_params=pltpu.CompilerParams(vmem_limit_bytes=4 * 1024 * 1024),
+        name="finish",
+    )(arrived)
+
+
 def summed(parts, axes):
     return jnp.sum(lax.all_to_all(parts, axes, 0, 0, tiled=True), axis=0)
 
@@ -245,10 +277,7 @@
     piece = summed(pieces, "y_far")
     copies = jnp.broadcast_to(piece, (groups, *piece.shape))
     arrived = lax.all_to_all(copies, GRP, 0, 0, tiled=True)
-    whole = jnp.sum(arrived.reshape(groups // 2, 2, *piece.shape), axis=0)
-    grads = whole[:, :-8].reshape(2, wide // 128, 8, 128).transpose(0, 2, 1, 3).reshape(2, 8, wide)
-    err_norms = jnp.sqrt(whole[0, -8 : steps - 8, 0] / row_count)
-    return (err_norms, grads[0], grads[1])
+    return finish(arrived, steps, wide, row_count)
 
 
 def solution(mesh):

time: 89.3 us -> 87.8 us (0.983)
  no operation moved by 1% of the time
where the time goes in v4:
time: 87.8 us; the launch traced here: 87.6 us
  blocking collectives  70.2 us (80%)
  Pallas kernels  10.2 us (12%)
  waiting for transfers between devices  4.22 us (5%)
  starting transfers between devices  1.92 us (2%)
    all_to_all x2, blocking collectives, summed(): return jnp.sum(lax.all_to_all(parts, axes, 0, 0, tiled=True), axis=0)  50.1 us
    all_to_all x1, blocking collectives, per_device(): arrived = lax.all_to_all(copies, GRP, 0, 0, tiled=True)  20 us
    pallas_call x1, Pallas kernels, run_steps(): pl.pallas_call(steps_kernel, out_shape=(half, half), in_specs=[smem] + [h...  9.53 us
    ppermute x1, waiting for transfers between devices, per_device(): mine = keep + lax.ppermute(send, 'core', [(0, 1), (1, 0)])  4.22 us
    ppermute x1, starting transfers between devices, per_device(): mine = keep + lax.ppermute(send, 'core', [(0, 1), (1, 0)])  1.92 us
  transfers between devices with their start and end apart: 1, of which 1 were waited for; matrix products, arithmetic and copies ran while one was open for 0% of the time, Pallas kernels for 0%

profile of v4, /device:TPU:8, one launch (start us, length us, event | category | flops | bytes accessed | tf_op | source)
XLA Modules:
  0.0 87.6 jit_solution(11190974509976292758)
XLA Ops:
  0.6 9.5 %milstein_steps.1 = (f32[16,264,128]{2,1,0:T(8,128)S(1)}, f32[16,264,128]{2,1,0:T(8,128)S(1)}) custom-call(s32[1]{0:T(128)} %bitcast.core_ref, bf16[128,512]{1,0:T(8,128)(2,1)} %start_hbm.1, bf16[512,1024]{1,0:T(8,128)(2,1)} %w_up_hbm.1, f32[1,1024]{1,0:T(1,128)} %bitcast.5, bf16[1024,512]{1,0:T(8,128)(2,1)} %w_down_hbm.1, bf16[512,1024]{1,0:T(8,128)(2,1)} %w_spread_hbm.1, ...), custom_call_target="tpu_custom_call" | custom-call | tf_op jit(solution)/shard_map/milstein_steps/pallas_call | solution.py:193
  10.2 1.9 %collective-permute-start = (f32[16,264,128]{2,1,0:T(8,128)S(1)}, f32[16,264,128]{2,1,0:T(8,128)S(1)}, u32[]{:S(2)}, u32[]{:S(2)}) collective-permute-start(f32[16,264,128]{2,1,0:T(8,128)S(1)} %get-tuple-element.6), channel_id=1, source_target_pairs={{0,1},{1,0},{2,3},{3,2},{4,5},{5,4},{6,7},{7,6},{8,9},{9,8},{10,11... | collective-permute-start | bytes 6488072 | tf_op jit(solution)/shard_map/ppermute | solution.py:272
  12.1 4.2 %collective-permute-done = f32[16,264,128]{2,1,0:T(8,128)S(1)} collective-permute-done((f32[16,264,128]{2,1,0:T(8,128)S(1)}, f32[16,264,128]{2,1,0:T(8,128)S(1)}, u32[]{:S(2)}, u32[]{:S(2)}) %collective-permute-start) | collective-permute-done | bytes 2162720 | tf_op jit(solution)/shard_map/ppermute | solution.py:272
  16.3 0.2 add.3
  16.5 36.3 %all_to_all.15 = f32[16,264,128]{2,1,0:T(8,128)S(1)} all-to-all(f32[16,264,128]{2,1,0:T(8,128)S(1)} %add.3), channel_id=1, replica_groups=mesh['z_far'=2,'z_mid'=2,'z_pair'=2,'y_far'=4,'y_pair'=2,'x'=4,'core'=2]..., dimensions={0} | all-to-all | bytes 4325376 | tf_op jit(solution)/shard_map/all_to_all | solution.py:255
  52.9 0.1 reduce_sum.18
  53.0 13.8 %all_to_all.16 = f32[4,72,128]{2,1,0:T(8,128)S(1)} all-to-all(f32[4,72,128]{2,1,0:T(8,128)S(1)} %pad_maximum_fusion), channel_id=1, replica_groups=mesh['z_far'=2,'z_mid'=2,'z_pair'=2,'y_far'=4,'y_pair'=2,'x'=4,'core'=2]..., dimensions={0} | all-to-all | bytes 294912 | tf_op jit(solution)/shard_map/all_to_all | solution.py:255
  66.9 20.0 %all_to_all.17.arrived_ref = f32[8,72,128]{2,1,0:T(8,128)S(1)} all-to-all(f32[8,72,128]{2,1,0:T(8,128)S(1)} %broadcast_in_dim.19), channel_id=1, replica_groups=mesh['z_far'=2,'z_mid'=2,'z_pair'=2,'y_far'=4,'y_pair'=2,'x'=4,'core'=2]..., dimensions={0} | all-to-all | bytes 589824 | tf_op jit(solution)/shard_map/all_to_all | solution.py:279
  86.9 0.6 finish.1
  (6 shorter events, 0.1 us)
Async XLA Ops:
  10.2 6.1 %collective-permute-start = (f32[16,264,128]{2,1,0:T(8,128)S(1)}, f32[16,264,128]{2,1,0:T(8,128)S(1)}, u32[]{:S(2)}, u32[]{:S(2)}) collective-permute-start(f32[16,264,128]{2,1,0:T(8,128)S(1)} %get-tuple-element.6), channel_id=1, source_target_pairs={{0,1},{1,0},{2,3},{3,2},{4,5},{5,4},{6,7},{7,6},{8,9},{9,8},{10,11... | collective-permute-start | bytes 6488072 | tf_op jit(solution)/shard_map/ppermute | solution.py:272
